TPU v7x, 128 devices: a whole 4x4x4 slice. The times are simulated.
128 devices in a mesh: gx: 16 (over z, y_lo, core), gy: 4 (over x), gz: 2 (over y_hi).
Axes of the slice: x: 4, y: 4 (y_hi: 2, y_lo: 2; y = y_hi * 2 + y_lo), z: 4, core: 2. Of those that a mesh axis runs over, the one named last changes fastest.
Arguments:
- models: float32 [2, 256, 128, 256], P(None, 'gx', 'gy', 'gz'), may hold values from -6 to 6
- targets: float32 [2, 256, 128, 256], P(None, 'gx', 'gy', 'gz'), may hold values from -6 to 6
- weights: float32 [2, 256, 128, 256], P(None, 'gx', 'gy', 'gz'), may hold values from 0.5 to 12, as said below
Outputs:
- updated: float32 [2, 256, 128, 256], P(None, 'gx', 'gy', 'gz')
- applied_last: float32 [2, 256, 128, 256], P(None, 'gx', 'gy', 'gz')
Inputs may be any that keep to these rules, and one draw needn't show every extreme that they name: Positive data weights.
All inputs are finite; a program needn't handle non-finite values.
Results may differ from a plain program's by a relative error of at most 0.00016.
Values sent between devices are 32-bit elements; how exact they have to be, the bound alone decides.
A program may use at most 128 MiB of HBM per device.

v0:
```python
import functools

import jax
import jax.numpy as jnp
from jax import lax
from jax.sharding import Mesh
from jax.sharding import PartitionSpec as P

ITERS = 3
GX_GY_GZ = ("gx_0", "gx_1", "gx_2", "gy", "gz")
GX = ("gx_0", "gx_1", "gx_2")


def padded_2(cells, sides, width):
    for axis, dim in sides:
        count = lax.axis_size(axis)
        ends = count - 1
        head = lax.slice_in_dim(cells, 0, width, axis=dim)
        tail = lax.slice_in_dim(cells, cells.shape[dim] - width, cells.shape[dim], axis=dim)
        cells = jnp.concatenate(
            [
                lax.ppermute(tail, axis, [(i, (i + 1) % count) for i in range(ends)]),
                cells,
                lax.ppermute(head, axis, [((i + 1) % count, i) for i in range(ends)]),
            ],
            axis=dim,
        )
    return cells


def one_axis_at_a_time(value, axes):
    return functools.reduce(lax.psum, axes, value)


def central_padded(padded, which):
    if which == 0:
        return 0.5 * (padded[2:, 1:-1, 1:-1] - padded[:-2, 1:-1, 1:-1])
    if which == 1:
        return 0.5 * (padded[1:-1, 2:, 1:-1] - padded[1:-1, :-2, 1:-1])
    return 0.5 * (padded[1:-1, 1:-1, 2:] - padded[1:-1, 1:-1, :-2])


def laplace_padded(padded):
    center = padded[1:-1, 1:-1, 1:-1]
    neighbours = padded[2:, 1:-1, 1:-1] + padded[:-2, 1:-1, 1:-1]
    neighbours = neighbours + padded[1:-1, 2:, 1:-1] + padded[1:-1, :-2, 1:-1]
    neighbours = neighbours + padded[1:-1, 1:-1, 2:] + padded[1:-1, 1:-1, :-2]
    return 6.0 * center - neighbours


def vector_cross(first_vec, second_vec):
    return (
        first_vec[1] * second_vec[2] - first_vec[2] * second_vec[1],
        first_vec[2] * second_vec[0] - first_vec[0] * second_vec[2],
        first_vec[0] * second_vec[1] - first_vec[1] * second_vec[0],
    )


def coupled_fields(padded_models):
    first_grad = [central_padded(padded_models[0], k) for k in range(3)]
    second_grad = [central_padded(padded_models[1], k) for k in range(3)]
    crossed = vector_cross(first_grad, second_grad)
    first_flux = vector_cross(second_grad, crossed)
    second_flux = vector_cross(crossed, first_grad)
    return jnp.stack(list(first_flux) + list(second_flux))


def coupling_terms(padded_fields):
    first_div = (
        central_padded(padded_fields[0], 0)
        + central_padded(padded_fields[1], 1)
        + central_padded(padded_fields[2], 2)
    )
    second_div = (
        central_padded(padded_fields[3], 0)
        + central_padded(padded_fields[4], 1)
        + central_padded(padded_fields[5], 2)
    )
    return -2.0 * jnp.stack([first_div, second_div])


def edge_keep(cells, device_pos, devices):
    position = jnp.arange(cells + 2)
    low_out = jnp.logical_and(position == 0, device_pos == 0)
    high_out = jnp.logical_and(position == cells + 1, device_pos == devices - 1)
    return jnp.logical_not(jnp.logical_or(low_out, high_out)).astype(jnp.float32)


def local(models, targets, weights):
    cells_x, cells_y, cells_z = (models.shape[1], models.shape[2], models.shape[3])
    current = models
    applied = jnp.zeros_like(models)
    for iteration in range(ITERS):
        deeper = padded_2(current, ((GX, 1), ("gy", 2), ("gz", 3)), 2)
        padded = deeper[:, 1:-1, 1:-1, 1:-1]
        rim_mask = (
            edge_keep(cells_x, lax.axis_index(GX), lax.axis_size(GX))[:, None, None]
            * edge_keep(cells_y, lax.axis_index("gy"), lax.axis_size("gy"))[None, :, None]
            * edge_keep(cells_z, lax.axis_index("gz"), lax.axis_size("gz"))[None, None, :]
        )
        padded_fields = coupled_fields(deeper) * rim_mask[None]
        smooth = jnp.stack([laplace_padded(padded[0]), laplace_padded(padded[1])])
        coupling = coupling_terms(padded_fields)
        gradient = weights * (current - targets) + 1.0 * smooth + 0.05 * coupling
        local_norm = jnp.sum(gradient * gradient)
        padded_grad = padded_2(gradient, ((GX, 1), ("gy", 2), ("gz", 3)), 1)
        applied = weights * gradient + 1.0 * jnp.stack(
            [laplace_padded(padded_grad[0]), laplace_padded(padded_grad[1])]
        )
        local_curv = jnp.sum(gradient * applied)
        grad_norm, curvature = (
            one_axis_at_a_time(local_norm, GX_GY_GZ),
            one_axis_at_a_time(local_curv, GX_GY_GZ),
        )
        step_size = grad_norm / curvature
        current = current - step_size * gradient
    return (current, applied)


def solution(mesh):
    finer = Mesh(
        mesh.devices.reshape(4, 2, 2, mesh.shape["gy"], mesh.shape["gz"]),
        ("gx_0", "gx_1", "gx_2", "gy", "gz"),
    )
    in_specs = (P(None, GX, "gy", "gz"), P(None, GX, "gy", "gz"), P(None, GX, "gy", "gz"))
    out_specs = (P(None, GX, "gy", "gz"), P(None, GX, "gy", "gz"))
    return jax.shard_map(local, mesh=finer, in_specs=in_specs, out_specs=out_specs, check_vma=False)
```

profile of v0, /device:TPU:16, one launch (start us, length us, event | category | flops | bytes accessed | tf_op | source)
XLA Modules:
  0.0 439.4 jit_solution(4943765046524625919)
XLA Ops:
  13.5 3.8 collective-permute-done.3
  24.9 6.1 %collective-permute-start.5 = (f32[2,20,36,2]{2,3,1,0:T(2,128)S(1)}, f32[2,20,36,2]{2,3,1,0:T(2,128)S(1)}, u32[]{:S(2)}, u32[]{:S(2)}) collective-permute-start(f32[2,20,36,2]{2,3,1,0:T(2,128)S(1)} %get-tuple-element.79), channel_id=1, source_target_pairs={{1,0},{3,2},{5,4},{7,6},{9,8},{11,10},{13,12},{15,14},{17,16},{19,... | collective-permute-start | bytes 34568 | tf_op jit(solution)/shard_map/ppermute | solution.py:24
  35.1 4.7 %fusion.63 = (f32[1,16,32,128]{2,3,1,0:T(8,128)}, f32[1,16,32,128]{2,3,1,0:T(8,128)}) fusion(f32[18,34,130]{1,2,0:T(8,128)S(1)} %get-tuple-element.115, f32[18,34,130]{1,2,0:T(8,128)S(1)} %get-tuple-element.114), kind=kLoop, calls=%fused_computation.232 | loop fusion | flops 917504 | bytes 4194304 | tf_op jit(solution)/shard_map/stack | solution.py:102
  43.5 4.7 %bitcast_dynamic-update-slice_fusion.17 = (f32[6,18,34,130]{2,3,1,0:T(8,128)}, f32[18,34,130]{1,2,0:T(8,128)S(1)}, f32[18,34,130]{1,2,0:T(8,128)S(1)}, f32[18,34...) fusion(f32[20,36,132]{1,2,0:T(8,128)S(1)} %get-tuple-element.11, ...), kind=kLoop, calls=%fused_computation.98 | loop fusion | flops 1670759 | bytes 7618176
  59.4 4.0 fusion.56
  70.0 5.6 %collective-permute-done.7 = f32[2,1,32,128]{3,2,1,0:T(8,128)S(1)} collective-permute-done((f32[2,1,32,128]{3,2,1,0:T(8,128)S(1)}, f32[2,1,32,128]{3,2,1,0:T(8,128)S(1)}, u32[]{:S(2)}, u32[]{:S(2)}) %collective-permute-start.7) | collective-permute-done | bytes 32800 | tf_op jit(solution)/shard_map/ppermute | solution.py:24
  88.5 5.3 %collective-permute-start.11 = (f32[2,18,34,1]{2,0,3,1:T(2,128)S(1)}, f32[2,18,34,1]{2,0,3,1:T(2,128)S(1)}, u32[]{:S(2)}, u32[]{:S(2)}) collective-permute-start(f32[2,18,34,1]{2,0,3,1:T(2,128)S(1)} %copy.100), channel_id=1, source_target_pairs={{1,0},{3,2},{5,4},{7,6},{9,8},{11,10},{13,12},{15,14},{17,16},{19,... | collective-permute-start | bytes 14696 | tf_op jit(solution)/shard_map/ppermute | solution.py:24
  95.5 5.4 %collective-permute-done.10 = f32[2,18,34,1]{2,0,3,1:T(2,128)S(1)} collective-permute-done((f32[2,18,34,1]{2,0,3,1:T(2,128)S(1)}, f32[2,18,34,1]{2,0,3,1:T(2,128)S(1)}, u32[]{:S(2)}, u32[]{:S(2)}) %collective-permute-start.10) | collective-permute-done | bytes 4928 | tf_op jit(solution)/shard_map/ppermute | solution.py:22
  108.2 16.4 %all-reduce.5 = (f32[]{:T(128)}, f32[]{:T(128)}) all-reduce(f32[]{:T(128)} %get-tuple-element.9, f32[]{:T(128)} %get-tuple-element.8), channel_id=1, replica_groups=mesh['gx_0'=4,'gx_1'=2,'gx_2'=2,'gy'=4,'gz'=2] {'gx_0'}, use_global_device_ids=true, to_apply=%region_1.0 | all-reduce | flops 2 | bytes 16 | tf_op jit(solution)/shard_map/psum | solution.py:32
  124.6 5.5 %all-reduce.14 = (f32[]{:T(128)}, f32[]{:T(128)}) all-reduce(f32[]{:T(128)} %get-tuple-element.20, f32[]{:T(128)} %get-tuple-element.21), channel_id=1, replica_groups=mesh['gx_0'=4,'gx_1'=2,'gx_2'=2,'gy'=4,'gz'=2] {'gx_1'}, use_global_device_ids=true, to_apply=%region_2.0 | all-reduce | flops 2 | bytes 16 | tf_op jit(solution)/shard_map/psum | solution.py:32
  133.2 10.6 %all-reduce.2 = (f32[]{:T(128)}, f32[]{:T(128)}) all-reduce(f32[]{:T(128)} %get-tuple-element.32, f32[]{:T(128)} %get-tuple-element.33), channel_id=1, replica_groups=mesh['gx_0'=4,'gx_1'=2,'gx_2'=2,'gy'=4,'gz'=2] {'gy'}, use_global_device_ids=true, to_apply=%region_4.0 | all-reduce | flops 2 | bytes 16 | tf_op jit(solution)/shard_map/psum | solution.py:32
  143.7 7.1 %all-reduce.8 = (f32[]{:T(128)}, f32[]{:T(128)}) all-reduce(f32[]{:T(128)} %get-tuple-element.14, f32[]{:T(128)} %get-tuple-element.15), channel_id=1, replica_groups=mesh['gx_0'=4,'gx_1'=2,'gx_2'=2,'gy'=4,'gz'=2] {'gz'}, use_global_device_ids=true, to_apply=%region_5.0 | all-reduce | flops 2 | bytes 16 | tf_op jit(solution)/shard_map/psum | solution.py:32
  158.4 4.5 %collective-permute-start.14 = (f32[2,20,2,128]{3,2,1,0:T(2,128)S(1)}, f32[2,20,2,128]{3,2,1,0:T(2,128)S(1)}, u32[]{:S(2)}, u32[]{:S(2)}) collective-permute-start(f32[2,20,2,128]{3,2,1,0:T(2,128)S(1)} %get-tuple-element.124), channel_id=1, source_target_pairs={{0,2},{2,4},{4,6},{1,3},{3,5},{5,7},{8,10},{10,12},{12,14},{9,11},... | collective-permute-start | bytes 122888 | tf_op jit(solution)/shard_map/ppermute | solution.py:22
  172.3 6.1 %collective-permute-start.17 = (f32[2,20,36,2]{2,3,1,0:T(2,128)S(1)}, f32[2,20,36,2]{2,3,1,0:T(2,128)S(1)}, u32[]{:S(2)}, u32[]{:S(2)}) collective-permute-start(f32[2,20,36,2]{2,3,1,0:T(2,128)S(1)} %get-tuple-element.77), channel_id=1, source_target_pairs={{1,0},{3,2},{5,4},{7,6},{9,8},{11,10},{13,12},{15,14},{17,16},{19,... | collective-permute-start | bytes 34568 | tf_op jit(solution)/shard_map/ppermute | solution.py:24
  192.7 7.6 %bitcast_dynamic-update-slice_fusion.11 = (f32[6,18,34,130]{2,3,1,0:T(8,128)S(1)}, f32[18,34,130]{1,2,0:T(8,128)S(1)}, f32[18,34,130]{1,2,0:T(8,128)S(1)}, f32[1...) fusion(f32[20,36,132]{1,2,0:T(8,128)} %get-tuple-element.109, ...), kind=kLoop, calls=%fused_computation.92 | loop fusion | flops 1670759 | bytes 15099264
  209.7 4.0 fusion.40
  236.0 5.3 %collective-permute-start.23 = (f32[2,18,34,1]{2,0,3,1:T(2,128)S(1)}, f32[2,18,34,1]{2,0,3,1:T(2,128)S(1)}, u32[]{:S(2)}, u32[]{:S(2)}) collective-permute-start(f32[2,18,34,1]{2,0,3,1:T(2,128)S(1)} %copy.118), channel_id=1, source_target_pairs={{1,0},{3,2},{5,4},{7,6},{9,8},{11,10},{13,12},{15,14},{17,16},{19,... | collective-permute-start | bytes 14696 | tf_op jit(solution)/shard_map/ppermute | solution.py:24
  242.9 5.6 %collective-permute-done.22 = f32[2,18,34,1]{2,0,3,1:T(2,128)S(1)} collective-permute-done((f32[2,18,34,1]{2,0,3,1:T(2,128)S(1)}, f32[2,18,34,1]{2,0,3,1:T(2,128)S(1)}, u32[]{:S(2)}, u32[]{:S(2)}) %collective-permute-start.22) | collective-permute-done | bytes 4928 | tf_op jit(solution)/shard_map/ppermute | solution.py:22
  255.9 13.0 %all-reduce.4 = (f32[]{:T(128)}, f32[]{:T(128)}) all-reduce(f32[]{:T(128)} %get-tuple-element.7, f32[]{:T(128)} %get-tuple-element.6), channel_id=1, replica_groups=mesh['gx_0'=4,'gx_1'=2,'gx_2'=2,'gy'=4,'gz'=2] {'gx_0'}, use_global_device_ids=true, to_apply=%region_13.0 | all-reduce | flops 2 | bytes 16 | tf_op jit(solution)/shard_map/psum | solution.py:32
  268.8 5.6 %all-reduce.13 = (f32[]{:T(128)}, f32[]{:T(128)}) all-reduce(f32[]{:T(128)} %get-tuple-element.18, f32[]{:T(128)} %get-tuple-element.19), channel_id=1, replica_groups=mesh['gx_0'=4,'gx_1'=2,'gx_2'=2,'gy'=4,'gz'=2] {'gx_1'}, use_global_device_ids=true, to_apply=%region_14.0 | all-reduce | flops 2 | bytes 16 | tf_op jit(solution)/shard_map/psum | solution.py:32
  277.5 10.6 %all-reduce.1 = (f32[]{:T(128)}, f32[]{:T(128)}) all-reduce(f32[]{:T(128)} %get-tuple-element.30, f32[]{:T(128)} %get-tuple-element.31), channel_id=1, replica_groups=mesh['gx_0'=4,'gx_1'=2,'gx_2'=2,'gy'=4,'gz'=2] {'gy'}, use_global_device_ids=true, to_apply=%region_16.0 | all-reduce | flops 2 | bytes 16 | tf_op jit(solution)/shard_map/psum | solution.py:32
  288.2 7.1 %all-reduce.7 = (f32[]{:T(128)}, f32[]{:T(128)}) all-reduce(f32[]{:T(128)} %get-tuple-element.12, f32[]{:T(128)} %get-tuple-element.13), channel_id=1, replica_groups=mesh['gx_0'=4,'gx_1'=2,'gx_2'=2,'gy'=4,'gz'=2] {'gz'}, use_global_device_ids=true, to_apply=%region_17.0 | all-reduce | flops 2 | bytes 16 | tf_op jit(solution)/shard_map/psum | solution.py:32
  302.8 4.5 %collective-permute-start.26 = (f32[2,20,2,128]{3,2,1,0:T(2,128)S(1)}, f32[2,20,2,128]{3,2,1,0:T(2,128)S(1)}, u32[]{:S(2)}, u32[]{:S(2)}) collective-permute-start(f32[2,20,2,128]{3,2,1,0:T(2,128)S(1)} %get-tuple-element.122), channel_id=1, source_target_pairs={{0,2},{2,4},{4,6},{1,3},{3,5},{5,7},{8,10},{10,12},{12,14},{9,11},... | collective-permute-start | bytes 122888 | tf_op jit(solution)/shard_map/ppermute | solution.py:22
  318.9 5.7 %collective-permute-done.28 = f32[2,20,36,2]{2,1,3,0:T(8,128)S(1)} collective-permute-done((f32[2,20,36,2]{2,1,3,0:T(8,128)S(1)}, f32[2,20,36,2]{2,1,3,0:T(8,128)S(1)}, u32[]{:S(2)}, u32[]{:S(2)}) %collective-permute-start.28) | collective-permute-done | bytes 11552 | tf_op jit(solution)/shard_map/ppermute | solution.py:22
  337.4 7.8 %bitcast_dynamic-update-slice_fusion.5 = (f32[6,18,34,130]{2,3,1,0:T(8,128)S(1)}, f32[18,34,130]{1,2,0:T(8,128)S(1)}, f32[18,34,130]{1,2,0:T(8,128)S(1)}, f32[18...) fusion(f32[20,36,132]{1,2,0:T(8,128)} %get-tuple-element.105, ...), kind=kLoop, calls=%fused_computation.86 | loop fusion | flops 1670759 | bytes 15099264
  354.6 4.0 fusion.24
  365.7 3.9 collective-permute-done.31
  383.9 5.6 %collective-permute-done.34 = f32[2,18,34,1]{2,0,3,1:T(2,128)S(1)} collective-permute-done((f32[2,18,34,1]{2,0,3,1:T(2,128)S(1)}, f32[2,18,34,1]{2,0,3,1:T(2,128)S(1)}, u32[]{:S(2)}, u32[]{:S(2)}) %collective-permute-start.34) | collective-permute-done | bytes 4928 | tf_op jit(solution)/shard_map/ppermute | solution.py:22
  397.5 13.2 %all-reduce.3 = (f32[]{:T(128)}, f32[]{:T(128)}) all-reduce(f32[]{:T(128)} %get-tuple-element.5, f32[]{:T(128)} %get-tuple-element.4), channel_id=1, replica_groups=mesh['gx_0'=4,'gx_1'=2,'gx_2'=2,'gy'=4,'gz'=2] {'gx_0'}, use_global_device_ids=true, to_apply=%region_25.0 | all-reduce | flops 2 | bytes 16 | tf_op jit(solution)/shard_map/psum | solution.py:32
  410.6 5.6 %all-reduce.12 = (f32[]{:T(128)}, f32[]{:T(128)}) all-reduce(f32[]{:T(128)} %get-tuple-element.16, f32[]{:T(128)} %get-tuple-element.17), channel_id=1, replica_groups=mesh['gx_0'=4,'gx_1'=2,'gx_2'=2,'gy'=4,'gz'=2] {'gx_1'}, use_global_device_ids=true, to_apply=%region_26.0 | all-reduce | flops 2 | bytes 16 | tf_op jit(solution)/shard_map/psum | solution.py:32
  419.4 10.6 %all-reduce = (f32[]{:T(128)}, f32[]{:T(128)}) all-reduce(f32[]{:T(128)} %get-tuple-element.28, f32[]{:T(128)} %get-tuple-element.29), channel_id=1, replica_groups=mesh['gx_0'=4,'gx_1'=2,'gx_2'=2,'gy'=4,'gz'=2] {'gy'}, use_global_device_ids=true, to_apply=%region_28.0 | all-reduce | flops 2 | bytes 16 | tf_op jit(solution)/shard_map/psum | solution.py:32
  429.9 7.1 %all-reduce.6 = (f32[]{:T(128)}, f32[]{:T(128)}) all-reduce(f32[]{:T(128)} %get-tuple-element.10, f32[]{:T(128)} %get-tuple-element.11), channel_id=1, replica_groups=mesh['gx_0'=4,'gx_1'=2,'gx_2'=2,'gy'=4,'gz'=2] {'gz'}, use_global_device_ids=true, to_apply=%region_29.0 | all-reduce | flops 2 | bytes 16 | tf_op jit(solution)/shard_map/psum | solution.py:32
  (290 shorter events, 216.7 us)
Async XLA Ops:
  1.5 6.3 %collective-permute-start.1 = (f32[2,2,32,128]{3,2,1,0:T(8,128)S(1)}, f32[2,2,32,128]{3,2,1,0:T(8,128)S(1)}, u32[]{:S(2)}, u32[]{:S(2)}) collective-permute-start(f32[2,2,32,128]{3,2,1,0:T(8,128)S(1)} %get-tuple-element.144), channel_id=1, source_target_pairs={{8,0},{16,8},{24,16},{32,24},{40,32},{48,40},{56,48},{64,56},{72,6... | collective-permute-start | bytes 196616 | tf_op jit(solution)/shard_map/ppermute | solution.py:24
  2.8 3.9 collective-permute-start
  7.9 11.8 %collective-permute-start.2 = (f32[2,20,2,128]{3,2,1,0:T(2,128)S(1)}, f32[2,20,2,128]{3,2,1,0:T(2,128)S(1)}, u32[]{:S(2)}, u32[]{:S(2)}) collective-permute-start(f32[2,20,2,128]{3,2,1,0:T(2,128)S(1)} %get-tuple-element.126), channel_id=1, source_target_pairs={{0,2},{2,4},{4,6},{1,3},{3,5},{5,7},{8,10},{10,12},{12,14},{9,11},... | collective-permute-start | bytes 122888 | tf_op jit(solution)/shard_map/ppermute | solution.py:22
  11.3 6.1 %collective-permute-start.3 = (f32[2,20,2,128]{3,2,1,0:T(2,128)S(1)}, f32[2,20,2,128]{3,2,1,0:T(2,128)S(1)}, u32[]{:S(2)}, u32[]{:S(2)}) collective-permute-start(f32[2,20,2,128]{3,2,1,0:T(2,128)S(1)} %get-tuple-element.127), channel_id=1, source_target_pairs={{2,0},{4,2},{6,4},{3,1},{5,3},{7,5},{10,8},{12,10},{14,12},{11,9},... | collective-permute-start | bytes 122888 | tf_op jit(solution)/shard_map/ppermute | solution.py:24
  23.5 8.8 %collective-permute-start.4 = (f32[2,20,36,2]{2,3,1,0:T(2,128)S(1)}, f32[2,20,36,2]{2,3,1,0:T(2,128)S(1)}, u32[]{:S(2)}, u32[]{:S(2)}) collective-permute-start(f32[2,20,36,2]{2,3,1,0:T(2,128)S(1)} %get-tuple-element.78), channel_id=1, source_target_pairs={{0,1},{2,3},{4,5},{6,7},{8,9},{10,11},{12,13},{14,15},{16,17},{18,... | collective-permute-start | bytes 34568 | tf_op jit(solution)/shard_map/ppermute | solution.py:22
  24.9 7.7 %collective-permute-start.5 = (f32[2,20,36,2]{2,3,1,0:T(2,128)S(1)}, f32[2,20,36,2]{2,3,1,0:T(2,128)S(1)}, u32[]{:S(2)}, u32[]{:S(2)}) collective-permute-start(f32[2,20,36,2]{2,3,1,0:T(2,128)S(1)} %get-tuple-element.79), channel_id=1, source_target_pairs={{1,0},{3,2},{5,4},{7,6},{9,8},{11,10},{13,12},{15,14},{17,16},{19,... | collective-permute-start | bytes 34568 | tf_op jit(solution)/shard_map/ppermute | solution.py:24
  68.7 6.9 %collective-permute-start.7 = (f32[2,1,32,128]{3,2,1,0:T(8,128)S(1)}, f32[2,1,32,128]{3,2,1,0:T(8,128)S(1)}, u32[]{:S(2)}, u32[]{:S(2)}) collective-permute-start(f32[2,1,32,128]{3,2,1,0:T(8,128)S(1)} %get-tuple-element.143), channel_id=1, source_target_pairs={{8,0},{16,8},{24,16},{32,24},{40,32},{48,40},{56,48},{64,56},{72,6... | collective-permute-start | bytes 98312 | tf_op jit(solution)/shard_map/ppermute | solution.py:24
  75.7 6.5 %collective-permute-start.8 = (f32[2,18,1,128]{3,0,2,1:T(2,128)S(1)}, f32[2,18,1,128]{3,0,2,1:T(2,128)S(1)}, u32[]{:S(2)}, u32[]{:S(2)}) collective-permute-start(f32[2,18,1,128]{3,0,2,1:T(2,128)S(1)} %copy.145), channel_id=1, source_target_pairs={{0,2},{2,4},{4,6},{1,3},{3,5},{5,7},{8,10},{10,12},{12,14},{9,11},... | collective-permute-start | bytes 55304 | tf_op jit(solution)/shard_map/ppermute | solution.py:22
  79.2 5.7 %collective-permute-start.9 = (f32[2,18,1,128]{3,0,2,1:T(2,128)S(1)}, f32[2,18,1,128]{3,0,2,1:T(2,128)S(1)}, u32[]{:S(2)}, u32[]{:S(2)}) collective-permute-start(f32[2,18,1,128]{3,0,2,1:T(2,128)S(1)} %copy.146), channel_id=1, source_target_pairs={{2,0},{4,2},{6,4},{3,1},{5,3},{7,5},{10,8},{12,10},{14,12},{11,9},... | collective-permute-start | bytes 55304 | tf_op jit(solution)/shard_map/ppermute | solution.py:24
  88.5 7.0 %collective-permute-start.11 = (f32[2,18,34,1]{2,0,3,1:T(2,128)S(1)}, f32[2,18,34,1]{2,0,3,1:T(2,128)S(1)}, u32[]{:S(2)}, u32[]{:S(2)}) collective-permute-start(f32[2,18,34,1]{2,0,3,1:T(2,128)S(1)} %copy.100), channel_id=1, source_target_pairs={{1,0},{3,2},{5,4},{7,6},{9,8},{11,10},{13,12},{15,14},{17,16},{19,... | collective-permute-start | bytes 14696 | tf_op jit(solution)/shard_map/ppermute | solution.py:24
  93.8 7.2 %collective-permute-start.10 = (f32[2,18,34,1]{2,0,3,1:T(2,128)S(1)}, f32[2,18,34,1]{2,0,3,1:T(2,128)S(1)}, u32[]{:S(2)}, u32[]{:S(2)}) collective-permute-start(f32[2,18,34,1]{2,0,3,1:T(2,128)S(1)} %copy.99), channel_id=1, source_target_pairs={{0,1},{2,3},{4,5},{6,7},{8,9},{10,11},{12,13},{14,15},{16,17},{18,... | collective-permute-start | bytes 14696 | tf_op jit(solution)/shard_map/ppermute | solution.py:22
  153.6 3.4 collective-permute-start.13
  157.0 7.7 %collective-permute-start.15 = (f32[2,20,2,128]{3,2,1,0:T(2,128)S(1)}, f32[2,20,2,128]{3,2,1,0:T(2,128)S(1)}, u32[]{:S(2)}, u32[]{:S(2)}) collective-permute-start(f32[2,20,2,128]{3,2,1,0:T(2,128)S(1)} %get-tuple-element.125), channel_id=1, source_target_pairs={{2,0},{4,2},{6,4},{3,1},{5,3},{7,5},{10,8},{12,10},{14,12},{11,9},... | collective-permute-start | bytes 122888 | tf_op jit(solution)/shard_map/ppermute | solution.py:24
  158.4 8.7 %collective-permute-start.14 = (f32[2,20,2,128]{3,2,1,0:T(2,128)S(1)}, f32[2,20,2,128]{3,2,1,0:T(2,128)S(1)}, u32[]{:S(2)}, u32[]{:S(2)}) collective-permute-start(f32[2,20,2,128]{3,2,1,0:T(2,128)S(1)} %get-tuple-element.124), channel_id=1, source_target_pairs={{0,2},{2,4},{4,6},{1,3},{3,5},{5,7},{8,10},{10,12},{12,14},{9,11},... | collective-permute-start | bytes 122888 | tf_op jit(solution)/shard_map/ppermute | solution.py:22
  170.9 7.5 %collective-permute-start.16 = (f32[2,20,36,2]{2,3,1,0:T(2,128)S(1)}, f32[2,20,36,2]{2,3,1,0:T(2,128)S(1)}, u32[]{:S(2)}, u32[]{:S(2)}) collective-permute-start(f32[2,20,36,2]{2,3,1,0:T(2,128)S(1)} %get-tuple-element.76), channel_id=1, source_target_pairs={{0,1},{2,3},{4,5},{6,7},{8,9},{10,11},{12,13},{14,15},{16,17},{18,... | collective-permute-start | bytes 34568 | tf_op jit(solution)/shard_map/ppermute | solution.py:22
  172.3 7.7 %collective-permute-start.17 = (f32[2,20,36,2]{2,3,1,0:T(2,128)S(1)}, f32[2,20,36,2]{2,3,1,0:T(2,128)S(1)}, u32[]{:S(2)}, u32[]{:S(2)}) collective-permute-start(f32[2,20,36,2]{2,3,1,0:T(2,128)S(1)} %get-tuple-element.77), channel_id=1, source_target_pairs={{1,0},{3,2},{5,4},{7,6},{9,8},{11,10},{13,12},{15,14},{17,16},{19,... | collective-permute-start | bytes 34568 | tf_op jit(solution)/shard_map/ppermute | solution.py:24
  216.7 4.5 %collective-permute-start.18 = (f32[2,1,32,128]{3,2,1,0:T(8,128)S(1)}, f32[2,1,32,128]{3,2,1,0:T(8,128)S(1)}, u32[]{:S(2)}, u32[]{:S(2)}) collective-permute-start(f32[2,1,32,128]{3,2,1,0:T(8,128)S(1)} %get-tuple-element.138), channel_id=1, source_target_pairs={{0,8},{8,16},{16,24},{24,32},{32,40},{40,48},{48,56},{56,64},{64,7... | collective-permute-start | bytes 98312 | tf_op jit(solution)/shard_map/ppermute | solution.py:22
  219.8 4.3 collective-permute-start.19
  224.2 5.6 %collective-permute-start.20 = (f32[2,18,1,128]{3,0,2,1:T(2,128)S(1)}, f32[2,18,1,128]{3,0,2,1:T(2,128)S(1)}, u32[]{:S(2)}, u32[]{:S(2)}) collective-permute-start(f32[2,18,1,128]{3,0,2,1:T(2,128)S(1)} %copy.147), channel_id=1, source_target_pairs={{0,2},{2,4},{4,6},{1,3},{3,5},{5,7},{8,10},{10,12},{12,14},{9,11},... | collective-permute-start | bytes 55304 | tf_op jit(solution)/shard_map/ppermute | solution.py:22
  226.7 5.7 %collective-permute-start.21 = (f32[2,18,1,128]{3,0,2,1:T(2,128)S(1)}, f32[2,18,1,128]{3,0,2,1:T(2,128)S(1)}, u32[]{:S(2)}, u32[]{:S(2)}) collective-permute-start(f32[2,18,1,128]{3,0,2,1:T(2,128)S(1)} %copy.148), channel_id=1, source_target_pairs={{2,0},{4,2},{6,4},{3,1},{5,3},{7,5},{10,8},{12,10},{14,12},{11,9},... | collective-permute-start | bytes 55304 | tf_op jit(solution)/shard_map/ppermute | solution.py:24
  236.0 6.9 %collective-permute-start.23 = (f32[2,18,34,1]{2,0,3,1:T(2,128)S(1)}, f32[2,18,34,1]{2,0,3,1:T(2,128)S(1)}, u32[]{:S(2)}, u32[]{:S(2)}) collective-permute-start(f32[2,18,34,1]{2,0,3,1:T(2,128)S(1)} %copy.118), channel_id=1, source_target_pairs={{1,0},{3,2},{5,4},{7,6},{9,8},{11,10},{13,12},{15,14},{17,16},{19,... | collective-permute-start | bytes 14696 | tf_op jit(solution)/shard_map/ppermute | solution.py:24
  241.4 7.2 %collective-permute-start.22 = (f32[2,18,34,1]{2,0,3,1:T(2,128)S(1)}, f32[2,18,34,1]{2,0,3,1:T(2,128)S(1)}, u32[]{:S(2)}, u32[]{:S(2)}) collective-permute-start(f32[2,18,34,1]{2,0,3,1:T(2,128)S(1)} %copy.117), channel_id=1, source_target_pairs={{0,1},{2,3},{4,5},{6,7},{8,9},{10,11},{12,13},{14,15},{16,17},{18,... | collective-permute-start | bytes 14696 | tf_op jit(solution)/shard_map/ppermute | solution.py:22
  298.0 3.4 collective-permute-start.25
  301.5 7.7 %collective-permute-start.27 = (f32[2,20,2,128]{3,2,1,0:T(2,128)S(1)}, f32[2,20,2,128]{3,2,1,0:T(2,128)S(1)}, u32[]{:S(2)}, u32[]{:S(2)}) collective-permute-start(f32[2,20,2,128]{3,2,1,0:T(2,128)S(1)} %get-tuple-element.123), channel_id=1, source_target_pairs={{2,0},{4,2},{6,4},{3,1},{5,3},{7,5},{10,8},{12,10},{14,12},{11,9},... | collective-permute-start | bytes 122888 | tf_op jit(solution)/shard_map/ppermute | solution.py:24
  302.8 8.7 %collective-permute-start.26 = (f32[2,20,2,128]{3,2,1,0:T(2,128)S(1)}, f32[2,20,2,128]{3,2,1,0:T(2,128)S(1)}, u32[]{:S(2)}, u32[]{:S(2)}) collective-permute-start(f32[2,20,2,128]{3,2,1,0:T(2,128)S(1)} %get-tuple-element.122), channel_id=1, source_target_pairs={{0,2},{2,4},{4,6},{1,3},{3,5},{5,7},{8,10},{10,12},{12,14},{9,11},... | collective-permute-start | bytes 122888 | tf_op jit(solution)/shard_map/ppermute | solution.py:22
  315.3 3.5 collective-permute-start.29
  317.1 7.5 %collective-permute-start.28 = (f32[2,20,36,2]{2,1,3,0:T(8,128)S(1)}, f32[2,20,36,2]{2,1,3,0:T(8,128)S(1)}, u32[]{:S(2)}, u32[]{:S(2)}) collective-permute-start(f32[2,20,36,2]{2,1,3,0:T(8,128)S(1)} %copy.126), channel_id=1, source_target_pairs={{0,1},{2,3},{4,5},{6,7},{8,9},{10,11},{12,13},{14,15},{16,17},{18,... | collective-permute-start | bytes 34568 | tf_op jit(solution)/shard_map/ppermute | solution.py:22
  361.5 4.1 collective-permute-start.30
  364.3 5.2 %collective-permute-start.31 = (f32[2,1,32,128]{3,2,1,0:T(8,128)S(1)}, f32[2,1,32,128]{3,2,1,0:T(8,128)S(1)}, u32[]{:S(2)}, u32[]{:S(2)}) collective-permute-start(f32[2,1,32,128]{3,2,1,0:T(8,128)S(1)} %get-tuple-element.135), channel_id=1, source_target_pairs={{8,0},{16,8},{24,16},{32,24},{40,32},{48,40},{56,48},{64,56},{72,6... | collective-permute-start | bytes 98312 | tf_op jit(solution)/shard_map/ppermute | solution.py:24
  369.6 5.0 %collective-permute-start.32 = (f32[2,18,1,128]{3,0,2,1:T(2,128)S(1)}, f32[2,18,1,128]{3,0,2,1:T(2,128)S(1)}, u32[]{:S(2)}, u32[]{:S(2)}) collective-permute-start(f32[2,18,1,128]{3,0,2,1:T(2,128)S(1)} %copy.149), channel_id=1, source_target_pairs={{0,2},{2,4},{4,6},{1,3},{3,5},{5,7},{8,10},{10,12},{12,14},{9,11},... | collective-permute-start | bytes 55304 | tf_op jit(solution)/shard_map/ppermute | solution.py:22
  371.6 5.7 %collective-permute-start.33 = (f32[2,18,1,128]{3,0,2,1:T(2,128)S(1)}, f32[2,18,1,128]{3,0,2,1:T(2,128)S(1)}, u32[]{:S(2)}, u32[]{:S(2)}) collective-permute-start(f32[2,18,1,128]{3,0,2,1:T(2,128)S(1)} %copy.150), channel_id=1, source_target_pairs={{2,0},{4,2},{6,4},{3,1},{5,3},{7,5},{10,8},{12,10},{14,12},{11,9},... | collective-permute-start | bytes 55304 | tf_op jit(solution)/shard_map/ppermute | solution.py:24
  382.3 7.2 %collective-permute-start.34 = (f32[2,18,34,1]{2,0,3,1:T(2,128)S(1)}, f32[2,18,34,1]{2,0,3,1:T(2,128)S(1)}, u32[]{:S(2)}, u32[]{:S(2)}) collective-permute-start(f32[2,18,34,1]{2,0,3,1:T(2,128)S(1)} %copy.139), channel_id=1, source_target_pairs={{0,1},{2,3},{4,5},{6,7},{8,9},{10,11},{12,13},{14,15},{16,17},{18,... | collective-permute-start | bytes 14696 | tf_op jit(solution)/shard_map/ppermute | solution.py:22
  (45 other events, 365.6 us)
where the time goes:
time: 448 us; the launch traced here: 439 us
  blocking collectives  122 us (27%)
  other arithmetic  105 us (23%)
  starting transfers between devices  83.4 us (19%)
  local copies, waits for them, and re-layouts  75.5 us (17%)
  waiting for transfers between devices  47.3 us (11%)
  between operations  6.17 us (1%)
    psum x15, blocking collectives, one_axis_at_a_time(): return functools.reduce(lax.psum, axes, value)  122 us
    ppermute x18, starting transfers between devices, padded_2(): lax.ppermute(tail, axis, [(i, (i + 1) % count) for i in range(ends)])  42 us
    ppermute x18, starting transfers between devices, padded_2(): lax.ppermute(head, axis, [((i + 1) % count, i) for i in range(ends)])  41.4 us
    unnamed x15, other arithmetic  28.1 us
    ppermute x18, waiting for transfers between devices, padded_2(): lax.ppermute(head, axis, [((i + 1) % count, i) for i in range(ends)])  24.1 us
    ppermute x18, waiting for transfers between devices, padded_2(): lax.ppermute(tail, axis, [(i, (i + 1) % count) for i in range(ends)])  23.3 us
    another operation x5, other arithmetic, coupling_terms(): return -2.0 * jnp.stack([first_div, second_div])  16.9 us
    another operation x5, other arithmetic, local(): smooth = jnp.stack([laplace_padded(padded[0]), laplace_padded(padded[1])])  15.4 us
  transfers between devices with their start and end apart: 36, of which 17 were waited for; matrix products, arithmetic and copies ran while one was open for 6% of the time, Pallas kernels for 0%

commit v1 on v0

v1 whole, which is shorter than its diff:
```python
import functools

import jax
import jax.numpy as jnp
from jax import lax
from jax.experimental import pallas as pl
from jax.experimental.pallas import tpu as pltpu
from jax.sharding import PartitionSpec as P

ITERS = 3
MESH = pl.DeviceIdType.MESH
MODELS = 2
XO = 2
YO = 8
UNROLL = 4
KAPPA = 0.05 * -2.0 * 0.5 * 0.125


def kernel(sizes, models, targets, weights, updated, applied_out,
           field, tgt, wgt, base, flux0, flux1, flux2, ghost2, near, far, far_rows,
           own1, got1, own2, got2, out_c, out_a,
           load_sem, store_sem, send_sem, recv_sem, send1, recv1, send2, recv2):
    nx, ny, nz = sizes
    _, cx, cy, cz = tgt.shape
    tiles = cy // 8
    gx, gy, gz = lax.axis_index("gx"), lax.axis_index("gy"), lax.axis_index("gz")

    offsets = [(0, 0, 1), (1, 0, 1), (-1, 0, 1), (0, 1, 1), (0, -1, 1),
               (1, 0, 0), (-1, 0, 0), (0, 1, 0), (0, -1, 0),
               (1, 1, 0), (1, -1, 0), (-1, 1, 0), (-1, -1, 0)]

    def there(ox, oy):
        ok = None
        for place, step, count in ((gx, ox, nx), (gy, oy, ny)):
            if step != 0:
                here = place < count - 1 if step > 0 else place > 0
                ok = here if ok is None else jnp.logical_and(ok, here)
        return ok

    def guarded(ok, action):
        if ok is None:
            action()
        else:
            pl.when(ok)(action)

    def face(k, ox, oy, depth):
        x_src = {1: pl.ds(XO + cx - depth, depth), -1: pl.ds(XO, depth), 0: pl.ds(XO, cx)}[ox]
        x_dst = {1: pl.ds(XO - depth, depth), -1: pl.ds(XO + cx, depth), 0: pl.ds(XO, cx)}[ox]
        y_src = {1: pl.ds(YO + cy - depth, depth), -1: pl.ds(YO, depth), 0: pl.ds(YO, cy)}[oy]
        y_dst = {1: pl.ds(YO - depth, depth), -1: pl.ds(YO + cy, depth), 0: pl.ds(YO, cy)}[oy]
        return field.at[k, x_src, :, y_src, :], field.at[k, x_dst, :, y_dst, :]

    def message(k, j, last):
        ox, oy, oz = offsets[j]
        if oz:
            src, dst = near.at[k], far.at[k, j]
        else:
            depth = 1 if last or (ox and oy) else 2
            src, dst = face(k, ox, oy, depth)
        return pltpu.make_async_remote_copy(
            src_ref=src, dst_ref=dst, send_sem=send_sem.at[k, j], recv_sem=recv_sem.at[k, j],
            device_id={"gx": gx + ox, "gy": gy + oy, "gz": gz + oz - 2 * oz * gz}, device_id_type=MESH)

    def used(last):
        return [j for j, (ox, oy, oz) in enumerate(offsets) if not last or abs(ox) + abs(oy) + oz == 1]

    def start_exchange(k, last=False):
        for j in used(last):
            guarded(there(offsets[j][0], offsets[j][1]), lambda j=j: message(k, j, last).start())

    def wait_exchange(k, last=False):
        for j in used(last):
            guarded(there(-offsets[j][0], -offsets[j][1]), lambda j=j: message(k, j, last).wait_recv())

    def wait_sends(k, last=False):
        for j in used(last):
            guarded(there(offsets[j][0], offsets[j][1]), lambda j=j: message(k, j, last).wait_send())

    group1 = [(c, s) for s in range(ny) for c in range(2) if (c, s) != (0, 0)]
    group2 = [(h, s) for s in range(nz) for h in range(nx // 2) if (h, s) != (0, 0)]

    def peer1(j):
        c, s = group1[j]
        core = lax.rem(gx, 2)
        return {"gx": gx + c - 2 * c * core, "gy": lax.rem(gy + s, ny), "gz": gz}

    def peer2(j):
        h, s = group2[j]
        return {"gx": lax.rem(gx + 2 * h, nx), "gy": gy, "gz": gz + s - 2 * s * gz}

    def stage(k, peers, peer, own, got, sends, recvs):
        return [pltpu.make_async_remote_copy(
            src_ref=own.at[k], dst_ref=got.at[k, j], send_sem=sends.at[k, j], recv_sem=recvs.at[k, j],
            device_id=peer(j), device_id_type=MESH) for j in range(len(peers))]

    loads = []
    for m in range(MODELS):
        loads.append(pltpu.make_async_copy(models.at[m], field.at[0, pl.ds(XO, cx), m, pl.ds(YO, cy), :], load_sem.at[m]))
    loads.append(pltpu.make_async_copy(targets, tgt, load_sem.at[2]))
    loads.append(pltpu.make_async_copy(weights, wgt, load_sem.at[3]))
    for copy in loads:
        copy.start()

    zero = jnp.zeros((8, cz), jnp.float32)
    rows = field.shape[3]

    def clear_planes(start):
        for k in range(ITERS + 1):
            for x in range(start, start + XO):
                for m in range(MODELS):
                    for r in range(0, rows, 8):
                        field[k, x, m, pl.ds(r, 8), :] = zero

    def clear_rows(start):
        def clear(x, _):
            for k in range(ITERS + 1):
                for m in range(MODELS):
                    field[k, x, m, pl.ds(start, 8), :] = zero
            return 0

        lax.fori_loop(0, cx + 2 * XO, clear, 0)

    def clear_far(j):
        for k in range(ITERS + 1):
            for m in range(MODELS):
                far[k, j, m] = zero

    pl.when(gx == 0)(lambda: (clear_planes(0), clear_far(1))[0])
    pl.when(gx == nx - 1)(lambda: (clear_planes(XO + cx), clear_far(2))[0])
    pl.when(gy == 0)(lambda: (clear_rows(0), clear_far(3))[0])
    pl.when(gy == ny - 1)(lambda: (clear_rows(rows - 8), clear_far(4))[0])

    barrier = pltpu.get_barrier_semaphore()
    expected = len(group1) + len(group2)
    for ox, oy, oz in offsets:
        ok = there(ox, oy)
        guarded(ok, lambda ox=ox, oy=oy, oz=oz: pl.semaphore_signal(
            barrier, 1, device_id={"gx": gx + ox, "gy": gy + oy, "gz": gz + oz - 2 * oz * gz}, device_id_type=MESH))
        expected = expected + (1 if ok is None else ok.astype(jnp.int32))
    for j in range(len(group1)):
        pl.semaphore_signal(barrier, 1, device_id=peer1(j), device_id_type=MESH)
    for j in range(len(group2)):
        pl.semaphore_signal(barrier, 1, device_id=peer2(j), device_id_type=MESH)


    lane = lax.broadcasted_iota(jnp.int32, (8, cz), 1)
    row = lax.broadcasted_iota(jnp.int32, (8, cz), 0)
    first, last_lane = lane == 0, lane == cz - 1
    ghost_lane = lane == jnp.where(gz == 0, 0, cz - 1)

    def turn(v, shift):
        if isinstance(shift, int):
            shift = shift % cz
            return v if shift == 0 else pltpu.roll(v, shift, 1)
        return pltpu.roll(v, shift, 1)

    def edge(packed, at):
        back = (2 * cz - at - 2 * gz) % cz if not isinstance(at, int) else lax.rem(2 * cz - at - 2 * gz, cz)
        return jnp.where(ghost_lane, turn(packed, back), 0.0)

    def z_pair(v, e):
        return turn(jnp.where(first, e, v), cz - 1), turn(jnp.where(last_lane, e, v), 1)

    def pack(acc, v, t, x):
        put = lax.rem(2 * cx * t + 2 * x + 2 - 2 * gz, cz)
        return jnp.where(lax.div(lane, 2) == cx * t + x, turn(v, put), acc)

    def at(k, x, m, r):
        return field[k, x + XO, m, pl.ds(YO + r, 8), :]

    def over_x(body, carry):
        def block(b, carry):
            for u in range(UNROLL):
                carry = body(b * UNROLL + u, carry)
            return carry

        return lax.fori_loop(0, cx // UNROLL, block, carry)

    def cross_part(a, b, i):
        j, l = (i + 1) % 3, (i + 2) % 3
        return a[j] * b[l] - a[l] * b[j]

    def flux_part(g1, g2, which):
        crossed = [None, None, None]
        for i in range(3):
            if which is None or i != which:
                crossed[i] = cross_part(g1, g2, i)
        parts = range(3) if which is None else [which]
        return [(cross_part(g2, crossed, i), cross_part(crossed, g1, i)) for i in parts]

    for copy in loads[:MODELS]:
        copy.wait()
    empty = (zero,) * MODELS

    def pack_plane(x, acc):
        acc = list(acc)
        for m in range(MODELS):
            for t in range(tiles):
                acc[m] = pack(acc[m], at(0, x, m, 8 * t), t, x)
        return tuple(acc)

    packed = over_x(pack_plane, empty)
    for m in range(MODELS):
        near[0, m] = packed[m]
    pl.semaphore_wait(barrier, expected)
    start_exchange(0)
    for copy in loads[MODELS:]:
        copy.wait()
    wait_exchange(0)

    for k in range(1, ITERS + 1):
        final = k == ITERS
        for x, keep, j in ((-1, gx > 0, 1), (cx, gx < nx - 1, 2)):
            for t in range(tiles):
                grads = []
                for m in range(MODELS):
                    up, down = z_pair(at(0, x, m, 8 * t), edge(far[0, j, m], 2 * cx * t + (2 * cx - 2 if x < 0 else 0)))
                    grads.append([at(0, x + 1, m, 8 * t) - at(0, x - 1, m, 8 * t),
                                  at(0, x, m, 8 * t + 1) - at(0, x, m, 8 * t - 1), up - down])
                parts = flux_part(grads[0], grads[1], 0)[0]
                for m in range(MODELS):
                    flux0[x + 1, m, pl.ds(8 * t, 8), :] = jnp.where(keep, parts[m], 0.0)

        top = row == 0
        for m in range(MODELS):
            below = turn(far[0, 3, m], 2 * cx)
            for t in range(tiles):
                tile = jnp.where(lane < 2 * cx, turn(far[0, 0, m], -2 * cx * t),
                                 jnp.where(lane < 4 * cx, turn(far[0, 2, m], 2 * cx - 2 * cx * t),
                                           turn(far[0, 1, m], -2 * cx * t - 2 * cx)))
                far_rows[m, pl.ds(YO + 8 * t, 8), :] = tile
            far_rows[m, pl.ds(YO - 1, 1), :] = below[7:8]
            far_rows[m, pl.ds(YO + cy, 1), :] = far[0, 4, m][0:1]

        sign = (1 - 2 * gz).astype(jnp.float32)
        for t in range(tiles):
            grads = []
            for m in range(MODELS):
                here = far_rows[m, pl.ds(YO + 8 * t, 8), :]
                inner = turn(near[0, m], -2 * cx * t)
                grads.append([turn(here, -2) - turn(here, 2),
                              far_rows[m, pl.ds(YO + 8 * t + 1, 8), :] - far_rows[m, pl.ds(YO + 8 * t - 1, 8), :],
                              sign * turn(here - inner, jnp.where(gz == 0, cz - 1, 1))])
            parts = flux_part(grads[0], grads[1], 2)[0]
            for m in range(MODELS):
                ghost2[m, pl.ds(8 * t, 8), :] = parts[m]

        beside = [jnp.where(top, far_rows[m, pl.ds(YO - 1, 8), :],
                            far_rows[m, pl.ds(YO + cy - 1, 8), :]) for m in range(MODELS)]
        keep_low, keep_high = gy > 0, gy < ny - 1

        def fluxes(x, carry):
            def ends(dx, m, dy):
                return jnp.where(top, at(0, x + dx, m, dy - 1), at(0, x + dx, m, cy - 1 + dy))

            grads = []
            for m in range(MODELS):
                up, down = z_pair(ends(0, m, 0), edge(beside[m], 2 * x))
                grads.append([ends(1, m, 0) - ends(-1, m, 0), ends(0, m, 1) - ends(0, m, -1), up - down])
            parts = flux_part(grads[0], grads[1], 1)[0]
            for m in range(MODELS):
                flux1[x, m, pl.ds(YO - 1, 1), :] = jnp.where(keep_low, parts[m][0:1], 0.0)
                flux1[x, m, pl.ds(YO + cy, 1), :] = jnp.where(keep_high, parts[m][1:2], 0.0)
            for t in range(tiles):
                grads = []
                for m in range(MODELS):
                    here = at(0, x, m, 8 * t)
                    up, down = z_pair(here, edge(far[0, 0, m], 2 * cx * t + 2 * x))
                    xp, xm = at(0, x + 1, m, 8 * t), at(0, x - 1, m, 8 * t)
                    yp, ym = at(0, x, m, 8 * t + 1), at(0, x, m, 8 * t - 1)
                    grads.append([xp - xm, yp - ym, up - down])
                    smooth = 6.0 * here - ((xp + xm) + (yp + ym) + (up + down))
                    misfit = wgt[m, x, pl.ds(8 * t, 8), :] * (here - tgt[m, x, pl.ds(8 * t, 8), :])
                    base[m, x, pl.ds(8 * t, 8), :] = misfit + smooth
                parts = flux_part(grads[0], grads[1], None)
                for m in range(MODELS):
                    flux0[x + 1, m, pl.ds(8 * t, 8), :] = parts[0][m]
                    flux1[x, m, pl.ds(YO + 8 * t, 8), :] = parts[1][m]
                    flux2[x, m, pl.ds(8 * t, 8), :] = parts[2][m]
            return carry

        over_x(fluxes, 0)

        def gradients(x, carry):
            norm, acc = carry[0], list(carry[1:])
            for t in range(tiles):
                for m in range(MODELS):
                    here = flux2[x, m, pl.ds(8 * t, 8), :]
                    up, down = z_pair(here, edge(ghost2[m, pl.ds(8 * t, 8), :], 2 * x))
                    div = (flux0[x + 2, m, pl.ds(8 * t, 8), :] - flux0[x, m, pl.ds(8 * t, 8), :]
                           + (flux1[x, m, pl.ds(YO + 8 * t + 1, 8), :] - flux1[x, m, pl.ds(YO + 8 * t - 1, 8), :])
                           + (up - down))
                    grad = base[m, x, pl.ds(8 * t, 8), :] + KAPPA * div
                    field[k, x + XO, m, pl.ds(YO + 8 * t, 8), :] = grad
                    norm = norm + grad * grad
                    acc[m] = pack(acc[m], grad, t, x)
            return (norm, *acc)

        norm, *packed = over_x(gradients, (zero, *empty))
        for m in range(MODELS):
            near[k, m] = packed[m]
        start_exchange(k, final)
        wait_exchange(k, final)

        def applies(x, curve):
            for t in range(tiles):
                for m in range(MODELS):
                    here = at(k, x, m, 8 * t)
                    up, down = z_pair(here, edge(far[k, 0, m], 2 * cx * t + 2 * x))
                    around = ((at(k, x + 1, m, 8 * t) + at(k, x - 1, m, 8 * t))
                              + (at(k, x, m, 8 * t + 1) + at(k, x, m, 8 * t - 1)) + (up + down))
                    applied = wgt[m, x, pl.ds(8 * t, 8), :] * here + (6.0 * here - around)
                    curve = curve + here * applied
                    if final:
                        out_a[m, x, pl.ds(8 * t, 8), :] = applied
            return curve

        curve = over_x(applies, zero)
        if final:
            store_a = pltpu.make_async_copy(out_a, applied_out, store_sem.at[0])
            store_a.start()

        def fold(v):
            return jnp.sum(v, axis=0, keepdims=True)

        own1[k - 1, pl.ds(0, 1), :] = fold(norm)
        own1[k - 1, pl.ds(1, 1), :] = fold(curve)
        copies1 = stage(k - 1, group1, peer1, own1, got1, send1, recv1)
        for copy in copies1:
            copy.start()
        total = own1[k - 1]
        for j, copy in enumerate(copies1):
            copy.wait_recv()
            total = total + got1[k - 1, j]
        own2[k - 1] = total
        copies2 = stage(k - 1, group2, peer2, own2, got2, send2, recv2)
        for copy in copies2:
            copy.start()
        for j, copy in enumerate(copies2):
            copy.wait_recv()
            total = total + got2[k - 1, j]
        sums = jnp.sum(total, axis=1, keepdims=True)
        alpha = jnp.broadcast_to(sums[0:1] / sums[1:2], (8, cz))

        if k == 1:
            wait_sends(0)
        wait_sends(k, final)
        for copy in copies1 + copies2:
            copy.wait_send()

        if final:
            def step(x, carry):
                for m in range(MODELS):
                    for t in range(tiles):
                        out_c[m, x, pl.ds(8 * t, 8), :] = at(0, x, m, 8 * t) - alpha * at(k, x, m, 8 * t)
                return carry

            over_x(step, 0)
        else:
            def step(x, carry):
                for m in range(MODELS):
                    for r in range(0, rows, 8):
                        field[0, x, m, pl.ds(r, 8), :] = (
                            field[0, x, m, pl.ds(r, 8), :] - alpha * field[k, x, m, pl.ds(r, 8), :])
                return carry

            lax.fori_loop(0, cx + 2 * XO, step, 0)
            for m in range(MODELS):
                near[0, m] = near[0, m] - alpha * near[k, m]
                for j in range(5):
                    far[0, j, m] = far[0, j, m] - alpha * far[k, j, m]

    store_c = pltpu.make_async_copy(out_c, updated, store_sem.at[1])
    store_c.start()
    store_a.wait()
    store_c.wait()


def solution(mesh):
    sizes = (mesh.shape["gx"], mesh.shape["gy"], mesh.shape["gz"])
    nx, ny, nz = sizes

    def local(models, targets, weights):
        _, cx, cy, cz = models.shape
        assert nz == 2 and nx % 2 == 0 and 2 * cx * (cy // 8) == cz
        f32 = jnp.float32
        block = (MODELS, cx, cy, cz)
        rows = YO + cy + 8
        peers1, peers2 = 2 * ny - 1, nx // 2 * nz - 1
        return pl.pallas_call(
            functools.partial(kernel, sizes),
            out_shape=[jax.ShapeDtypeStruct(models.shape, f32)] * 2,
            in_specs=[pl.BlockSpec(memory_space=pl.ANY)] * 3,
            out_specs=[pl.BlockSpec(memory_space=pl.ANY)] * 2,
            scratch_shapes=[
                pltpu.VMEM((ITERS + 1, cx + 2 * XO, MODELS, rows, cz), f32),
                pltpu.VMEM(block, f32),
                pltpu.VMEM(block, f32),
                pltpu.VMEM(block, f32),
                pltpu.VMEM((cx + 2, MODELS, cy, cz), f32),
                pltpu.VMEM((cx, MODELS, rows, cz), f32),
                pltpu.VMEM((cx, MODELS, cy, cz), f32),
                pltpu.VMEM((MODELS, cy, cz), f32),
                pltpu.VMEM((ITERS + 1, MODELS, 8, cz), f32),
                pltpu.VMEM((ITERS + 1, 5, MODELS, 8, cz), f32),
                pltpu.VMEM((MODELS, rows, cz), f32),
                pltpu.VMEM((ITERS, 2, cz), f32),
                pltpu.VMEM((ITERS, peers1, 2, cz), f32),
                pltpu.VMEM((ITERS, 2, cz), f32),
                pltpu.VMEM((ITERS, peers2, 2, cz), f32),
                pltpu.VMEM(block, f32),
                pltpu.VMEM(block, f32),
                pltpu.SemaphoreType.DMA((4,)),
                pltpu.SemaphoreType.DMA((2,)),
                pltpu.SemaphoreType.DMA((ITERS + 1, 13)),
                pltpu.SemaphoreType.DMA((ITERS + 1, 13)),
                pltpu.SemaphoreType.DMA((ITERS, peers1)),
                pltpu.SemaphoreType.DMA((ITERS, peers1)),
                pltpu.SemaphoreType.DMA((ITERS, peers2)),
                pltpu.SemaphoreType.DMA((ITERS, peers2)),
            ],
            compiler_params=pltpu.CompilerParams(
                collective_id=0, has_side_effects=True, vmem_limit_bytes=60 * 2**20),
        )(models, targets, weights)

    spec = P(None, "gx", "gy", "gz")
    return jax.shard_map(local, mesh=mesh, in_specs=(spec,) * 3, out_specs=(spec,) * 2, check_vma=False)
```

time: 448 us -> 64.5 us (0.14)
  the two profiles are of different devices: /device:TPU:16 before, /device:TPU:1 now
where the time goes in v1:
time: 64.5 us; the launch traced here: 64.4 us
  Pallas kernels  61 us (95%)
  local copies, waits for them, and re-layouts  2.72 us (4%)
  between operations  0.65 us (1%)
    pallas_call x1, Pallas kernels, local(): pl.pallas_call(functools.partial(kernel, sizes), out_shape=[jax.ShapeDtyp...  61 us
    unnamed x4, local copies, waits for them, and re-layouts  2.72 us

profile of v1, /device:TPU:1, one launch (start us, length us, event | category | flops | bytes accessed | tf_op | source)
XLA Modules:
  0.0 64.4 jit_solution(12990036819034518387)
XLA Ops:
  0.6 61.0 %shard_map.50 = (f32[2,16,32,128]{3,2,1,0:T(8,128)}, f32[2,16,32,128]{3,2,1,0:T(8,128)}) custom-call(f32[2,16,32,128]{3,2,1,0:T(8,128)} %models.1, f32[2,16,32,128]{3,2,1,0:T(8,128)} %targets.1, f32[2,16,32,128]{3,2,1,0:T(8,128)} %weights.1), custom_call_target="tpu_custom_call" | custom-call | tf_op jit(solution)/shard_map/pallas_call | solution.py:390
  61.7 0.0 copy-start
  61.7 1.9 %copy.7 = f32[2,16,32,128]{3,2,1,0:T(8,128)} copy(f32[2,16,32,128]{3,2,1,0:T(8,128)} %get-tuple-element.4) | data formatting | bytes 1048576
  63.6 0.0 copy-done
  63.6 0.8 %copy.8 = f32[2,16,32,128]{3,2,1,0:T(8,128)} copy(f32[2,16,32,128]{3,2,1,0:T(8,128)S(1)} %copy-done) | data formatting | bytes 1048576
Async XLA Ops:
  61.7 1.9 %copy-start = (f32[2,16,32,128]{3,2,1,0:T(8,128)S(1)}, f32[2,16,32,128]{3,2,1,0:T(8,128)}, u32[]{:S(2)}) copy-start(f32[2,16,32,128]{3,2,1,0:T(8,128)} %get-tuple-element.5) | copy-start | bytes 1572868

commit v2 on v1

--- a/solution.py
+++ b/solution.py
@@ -18,8 +18,8 @@
 
 def kernel(sizes, models, targets, weights, updated, applied_out,
            field, tgt, wgt, base, flux0, flux1, flux2, ghost2, near, far, far_rows,
-           own1, got1, own2, got2, out_c, out_a,
-           load_sem, store_sem, send_sem, recv_sem, send1, recv1, send2, recv2):
+           own, got,
+           load_sem, send_sem, recv_sem, sum_send, sum_recv, enter_sem):
     nx, ny, nz = sizes
     _, cx, cy, cz = tgt.shape
     tiles = cy // 8
@@ -76,22 +76,36 @@
         for j in used(last):
             guarded(there(offsets[j][0], offsets[j][1]), lambda j=j: message(k, j, last).wait_send())
 
-    group1 = [(c, s) for s in range(ny) for c in range(2) if (c, s) != (0, 0)]
-    group2 = [(h, s) for s in range(nz) for h in range(nx // 2) if (h, s) != (0, 0)]
-
-    def peer1(j):
-        c, s = group1[j]
-        core = lax.rem(gx, 2)
-        return {"gx": gx + c - 2 * c * core, "gy": lax.rem(gy + s, ny), "gz": gz}
-
-    def peer2(j):
-        h, s = group2[j]
-        return {"gx": lax.rem(gx + 2 * h, nx), "gy": gy, "gz": gz + s - 2 * s * gz}
-
-    def stage(k, peers, peer, own, got, sends, recvs):
-        return [pltpu.make_async_remote_copy(
-            src_ref=own.at[k], dst_ref=got.at[k, j], send_sem=sends.at[k, j], recv_sem=recvs.at[k, j],
-            device_id=peer(j), device_id_type=MESH) for j in range(len(peers))]
+    others = [(x, y, z) for z in range(nz) for y in range(ny) for x in range(nx) if (x, y, z) != (0, 0, 0)]
+
+    def peer(x, y, z):
+        return {"gx": lax.rem(gx + x, nx) if x else gx, "gy": lax.rem(gy + y, ny) if y else gy,
+                "gz": lax.rem(gz + z, nz) if z else gz}
+
+    def start_sum(k):
+        for j, offset in enumerate(others):
+            pltpu.make_async_remote_copy(
+                src_ref=own.at[k], dst_ref=got.at[k, j], send_sem=sum_send.at[k], recv_sem=sum_recv.at[k],
+                device_id=peer(*offset), device_id_type=MESH).start()
+
+    def whole_sum(k):
+        return pltpu.make_async_remote_copy(
+            src_ref=got.at[k], dst_ref=got.at[k], send_sem=sum_send.at[k], recv_sem=sum_recv.at[k],
+            device_id=peer(1, 0, 0), device_id_type=MESH)
+
+    def on_line(x, y, z):
+        return {"gx": x, "gy": y, "gz": z}
+
+    pair, quad, chip_z = lax.rem(gx, 2), lax.rem(lax.div(gx, 2), 2), lax.div(gx, 4)
+    line_x = [on_line(gx + c - 2 * c * pair, lax.rem(gy + s, ny), gz)
+              for s in range(ny) for c in range(2) if (c, s) != (0, 0)]
+    line_y = [on_line(gx + 2 * h - 4 * h * quad, gy, gz + s - 2 * s * gz)
+              for s in range(nz) for h in range(2) if (h, s) != (0, 0)]
+    line_z = [on_line(lax.rem(gx + 4 * s, nx), gy, gz) for s in range(1, nx // 4)]
+
+    def tell(sem, line):
+        for device in line:
+            pl.semaphore_signal(sem, 1, device_id=device, device_id_type=MESH)
 
     loads = []
     for m in range(MODELS):
@@ -131,17 +145,14 @@
     pl.when(gy == ny - 1)(lambda: (clear_rows(rows - 8), clear_far(4))[0])
 
     barrier = pltpu.get_barrier_semaphore()
-    expected = len(group1) + len(group2)
+    expected = len(line_x) + len(line_y) + len(line_z)
     for ox, oy, oz in offsets:
         ok = there(ox, oy)
         guarded(ok, lambda ox=ox, oy=oy, oz=oz: pl.semaphore_signal(
             barrier, 1, device_id={"gx": gx + ox, "gy": gy + oy, "gz": gz + oz - 2 * oz * gz}, device_id_type=MESH))
         expected = expected + (1 if ok is None else ok.astype(jnp.int32))
-    for j in range(len(group1)):
-        pl.semaphore_signal(barrier, 1, device_id=peer1(j), device_id_type=MESH)
-    for j in range(len(group2)):
-        pl.semaphore_signal(barrier, 1, device_id=peer2(j), device_id_type=MESH)
-
+    for line in (line_x, line_y, line_z):
+        tell(barrier, line)
 
     lane = lax.broadcasted_iota(jnp.int32, (8, cz), 1)
     row = lax.broadcasted_iota(jnp.int32, (8, cz), 0)
@@ -204,9 +215,12 @@
         near[0, m] = packed[m]
     pl.semaphore_wait(barrier, expected)
     start_exchange(0)
+    tell(enter_sem.at[0], line_y)
     for copy in loads[MODELS:]:
         copy.wait()
     wait_exchange(0)
+    pl.semaphore_wait(enter_sem.at[0], len(line_y))
+    tell(enter_sem.at[1], line_z)
 
     for k in range(1, ITERS + 1):
         final = k == ITERS
@@ -312,47 +326,37 @@
                     applied = wgt[m, x, pl.ds(8 * t, 8), :] * here + (6.0 * here - around)
                     curve = curve + here * applied
                     if final:
-                        out_a[m, x, pl.ds(8 * t, 8), :] = applied
+                        applied_out[m, x, pl.ds(8 * t, 8), :] = applied
             return curve
 
         curve = over_x(applies, zero)
-        if final:
-            store_a = pltpu.make_async_copy(out_a, applied_out, store_sem.at[0])
-            store_a.start()
 
         def fold(v):
             return jnp.sum(v, axis=0, keepdims=True)
 
-        own1[k - 1, pl.ds(0, 1), :] = fold(norm)
-        own1[k - 1, pl.ds(1, 1), :] = fold(curve)
-        copies1 = stage(k - 1, group1, peer1, own1, got1, send1, recv1)
-        for copy in copies1:
-            copy.start()
-        total = own1[k - 1]
-        for j, copy in enumerate(copies1):
-            copy.wait_recv()
-            total = total + got1[k - 1, j]
-        own2[k - 1] = total
-        copies2 = stage(k - 1, group2, peer2, own2, got2, send2, recv2)
-        for copy in copies2:
-            copy.start()
-        for j, copy in enumerate(copies2):
-            copy.wait_recv()
-            total = total + got2[k - 1, j]
+        own[k - 1, pl.ds(0, 1), :] = fold(norm)
+        own[k - 1, pl.ds(1, 1), :] = fold(curve)
+        if k == 1:
+            pl.semaphore_wait(enter_sem.at[1], len(line_z))
+        start_sum(k - 1)
+        whole_sum(k - 1).wait_recv()
+        partial = [own[k - 1]] + [got[k - 1, j] for j in range(len(others))]
+        while len(partial) > 1:
+            partial = [sum(partial[i:i + 2]) for i in range(0, len(partial), 2)]
+        total = partial[0]
         sums = jnp.sum(total, axis=1, keepdims=True)
         alpha = jnp.broadcast_to(sums[0:1] / sums[1:2], (8, cz))
 
         if k == 1:
             wait_sends(0)
         wait_sends(k, final)
-        for copy in copies1 + copies2:
-            copy.wait_send()
+        whole_sum(k - 1).wait_send()
 
         if final:
             def step(x, carry):
                 for m in range(MODELS):
                     for t in range(tiles):
-                        out_c[m, x, pl.ds(8 * t, 8), :] = at(0, x, m, 8 * t) - alpha * at(k, x, m, 8 * t)
+                        updated[m, x, pl.ds(8 * t, 8), :] = at(0, x, m, 8 * t) - alpha * at(k, x, m, 8 * t)
                 return carry
 
             over_x(step, 0)
@@ -370,11 +374,6 @@
                 for j in range(5):
                     far[0, j, m] = far[0, j, m] - alpha * far[k, j, m]
 
-    store_c = pltpu.make_async_copy(out_c, updated, store_sem.at[1])
-    store_c.start()
-    store_a.wait()
-    store_c.wait()
-
 
 def solution(mesh):
     sizes = (mesh.shape["gx"], mesh.shape["gy"], mesh.shape["gz"])
@@ -382,16 +381,16 @@
 
     def local(models, targets, weights):
         _, cx, cy, cz = models.shape
-        assert nz == 2 and nx % 2 == 0 and 2 * cx * (cy // 8) == cz
+        assert nz == 2 and nx % 4 == 0 and 2 * cx * (cy // 8) == cz
         f32 = jnp.float32
         block = (MODELS, cx, cy, cz)
         rows = YO + cy + 8
-        peers1, peers2 = 2 * ny - 1, nx // 2 * nz - 1
+        others = nx * ny * nz - 1
         return pl.pallas_call(
             functools.partial(kernel, sizes),
             out_shape=[jax.ShapeDtypeStruct(models.shape, f32)] * 2,
-            in_specs=[pl.BlockSpec(memory_space=pl.ANY)] * 3,
-            out_specs=[pl.BlockSpec(memory_space=pl.ANY)] * 2,
+            in_specs=[pl.BlockSpec(memory_space=pltpu.HBM)] * 3,
+            out_specs=[pl.BlockSpec(memory_space=pltpu.VMEM)] * 2,
             scratch_shapes=[
                 pltpu.VMEM((ITERS + 1, cx + 2 * XO, MODELS, rows, cz), f32),
                 pltpu.VMEM(block, f32),
@@ -405,23 +404,17 @@
                 pltpu.VMEM((ITERS + 1, 5, MODELS, 8, cz), f32),
                 pltpu.VMEM((MODELS, rows, cz), f32),
                 pltpu.VMEM((ITERS, 2, cz), f32),
-                pltpu.VMEM((ITERS, peers1, 2, cz), f32),
-                pltpu.VMEM((ITERS, 2, cz), f32),
-                pltpu.VMEM((ITERS, peers2, 2, cz), f32),
-                pltpu.VMEM(block, f32),
-                pltpu.VMEM(block, f32),
+                pltpu.VMEM((ITERS, others, 2, cz), f32),
                 pltpu.SemaphoreType.DMA((4,)),
-                pltpu.SemaphoreType.DMA((2,)),
                 pltpu.SemaphoreType.DMA((ITERS + 1, 13)),
                 pltpu.SemaphoreType.DMA((ITERS + 1, 13)),
-                pltpu.SemaphoreType.DMA((ITERS, peers1)),
-                pltpu.SemaphoreType.DMA((ITERS, peers1)),
-                pltpu.SemaphoreType.DMA((ITERS, peers2)),
-                pltpu.SemaphoreType.DMA((ITERS, peers2)),
+                pltpu.SemaphoreType.DMA((ITERS,)),
+                pltpu.SemaphoreType.DMA((ITERS,)),
+                pltpu.SemaphoreType.REGULAR((2,)),
             ],
             compiler_params=pltpu.CompilerParams(
-                collective_id=0, has_side_effects=True, vmem_limit_bytes=60 * 2**20),
-        )(models, targets, weights)
+                collective_id=0, has_side_effects=True, vmem_limit_bytes=24 * 2**20),
+        )(*[pltpu.with_memory_space_constraint(a, pltpu.HBM) for a in (models, targets, weights)])
 
     spec = P(None, "gx", "gy", "gz")
     return jax.shard_map(local, mesh=mesh, in_specs=(spec,) * 3, out_specs=(spec,) * 2, check_vma=False)

time: 64.5 us -> 58 us (0.90)
  Pallas kernels: 61 us -> 55.7 us
  local copies, waits for them, and re-layouts: 2.72 us -> 1.59 us
    pallas_call x1, Pallas kernels: 61 us -> 55.7 us  [local(): pl.pallas_call(functools.partial(kernel, sizes), out_shape=[jax.ShapeDtyp...]
    unnamed x4 -> x2, local copies, waits for them, and re-layouts: 2.72 us -> 1.59 us
where the time goes in v2:
time: 58 us; the launch traced here: 57.9 us
  Pallas kernels  55.7 us (96%)
  local copies, waits for them, and re-layouts  1.59 us (3%)
  between operations  0.64 us (1%)
    pallas_call x1, Pallas kernels, local(): pl.pallas_call(functools.partial(kernel, sizes), out_shape=[jax.ShapeDtyp...  55.7 us
    unnamed x2, local copies, waits for them, and re-layouts  1.59 us

profile of v2, /device:TPU:1, one launch (start us, length us, event | category | flops | bytes accessed | tf_op | source)
XLA Modules:
  0.0 57.9 jit_solution(13066088069439026470)
XLA Ops:
  0.6 55.7 %shard_map.50 = (f32[2,16,32,128]{3,2,1,0:T(8,128)S(1)}, f32[2,16,32,128]{3,2,1,0:T(8,128)S(1)}) custom-call(f32[2,16,32,128]{3,2,1,0:T(8,128)} %models.1, f32[2,16,32,128]{3,2,1,0:T(8,128)} %targets.1, f32[2,16,32,128]{3,2,1,0:T(8,128)} %weights.1), custom_call_target="tpu_custom_call" | custom-call | tf_op jit(solution)/shard_map/pallas_call | solution.py:389
  56.3 0.8 %copy.7 = f32[2,16,32,128]{3,2,1,0:T(8,128)} copy(f32[2,16,32,128]{3,2,1,0:T(8,128)S(1)} %get-tuple-element.4) | data formatting | bytes 1048576
  57.1 0.8 %copy.8 = f32[2,16,32,128]{3,2,1,0:T(8,128)} copy(f32[2,16,32,128]{3,2,1,0:T(8,128)S(1)} %get-tuple-element.5) | data formatting | bytes 1048576

commit v3 on v2

v3 whole, which is shorter than its diff:
```python
import functools

import jax
import jax.numpy as jnp
from jax import lax
from jax.experimental import pallas as pl
from jax.experimental.pallas import tpu as pltpu
from jax.sharding import PartitionSpec as P

ITERS = 3
MESH = pl.DeviceIdType.MESH
MODELS = 2
XO = 2
YO = 8
LOW, HIGH = 2, 3
SPAN = 5
UNROLL = 4
KAPPA = 0.05 * -2.0 * 0.5 * 0.125


def kernel(sizes, models, targets, weights, updated, applied_out,
           field, tgt, wgt, base, flux0, flux1, flux2, z_own, z_got, z_field, z_flux, z_grad, z_fixed,
           x_own, x_got, corner, own, got,
           load_sem, send_sem, recv_sem, fixed_send, fixed_recv, sum_send, sum_recv, enter_sem):
    nx, ny, nz = sizes
    _, cx, cy, cz = updated.shape
    tiles = cy // 8
    rows = field.shape[3]
    wide = tiles + 1
    gx, gy, gz = lax.axis_index("gx"), lax.axis_index("gy"), lax.axis_index("gz")

    faces = [(1, 0, 0), (-1, 0, 0), (0, 1, 0), (0, -1, 0), (1, 1, 0), (1, -1, 0), (-1, 1, 0), (-1, -1, 0)]
    z_faces = [(0, 0, 1), (1, 0, 0), (-1, 0, 0), (1, 0, 1), (-1, 0, 1), (0, 1, 0), (0, -1, 0), (0, 1, 1), (0, -1, 1),
               (1, 1, 1), (1, -1, 1), (-1, 1, 1), (-1, -1, 1)]
    corners = z_faces[9:]

    def there(ox, oy):
        ok = None
        for place, step, count in ((gx, ox, nx), (gy, oy, ny)):
            if step != 0:
                here = place < count - 1 if step > 0 else place > 0
                ok = here if ok is None else jnp.logical_and(ok, here)
        return ok

    def guarded(ok, action):
        if ok is None:
            action()
        else:
            pl.when(ok)(action)

    def device(ox, oy, oz):
        return {"gx": gx + ox, "gy": gy + oy, "gz": gz + oz - 2 * oz * gz}

    def slices(step, offset, count, skip, depth):
        if step > 0:
            return pl.ds(offset + count - LOW, LOW), pl.ds(offset - LOW, LOW)
        if step < 0:
            return pl.ds(offset + skip, depth - skip), pl.ds(offset + count + skip, depth - skip)
        return pl.ds(offset, count), pl.ds(offset, count)

    def message(k, j, last=False):
        if j < len(faces):
            ox, oy, oz = faces[j]
            if last:
                x_src, x_dst = (pl.ds(XO + cx - 1, 1), pl.ds(XO - 1, 1)) if ox else (pl.ds(XO, cx),) * 2
                y_src, y_dst = (pl.ds(YO + cy - 1, 1), pl.ds(YO - 1, 1)) if oy else (pl.ds(YO, cy),) * 2
            else:
                edge_of = ox != 0 and oy != 0
                skip, depth = (0, 2) if edge_of else (0 if k == 0 else 1, HIGH)
                x_src, x_dst = slices(ox, XO, cx, skip, depth)
                y_src, y_dst = slices(oy, YO, cy, skip, depth)
            src, dst = field.at[k, x_src, :, y_src, :], field.at[k, x_dst, :, y_dst, :]
        else:
            ox, oy, oz = offset = z_faces[j - len(faces)]
            y_src, y_dst = slices(oy, YO, cy, 0, 2)
            into = z_got if oz else z_own
            if ox and oy:
                line = YO + cy - 1 if oy > 0 else YO
                src, dst = z_own.at[k, :, pl.ds(line, 1), :], corner.at[k, corners.index(offset), :, pl.ds(0, 1), :]
            elif ox:
                src, dst = x_own.at[k, 0 if ox > 0 else 1], x_got.at[k, 0 if ox > 0 else 1, oz]
            else:
                src, dst = z_own.at[k, :, y_src, :], into.at[k, :, y_dst, :]
        return pltpu.make_async_remote_copy(
            src_ref=src, dst_ref=dst, send_sem=send_sem.at[k, j], recv_sem=recv_sem.at[k, j],
            device_id=device(ox, oy, oz), device_id_type=MESH)

    everything = faces + z_faces
    plain = list(range(len(faces)))
    through_z = list(range(len(faces), len(everything)))

    def start_copies(k, which, last=False):
        for j in which:
            guarded(there(*everything[j][:2]), lambda j=j: message(k, j, last).start())

    def wait_copies(k, which, last=False):
        for j in which:
            ox, oy, _ = everything[j]
            guarded(there(-ox, -oy), lambda j=j: message(k, j, last).wait_recv())

    def wait_sent(k, which, last=False):
        for j in which:
            guarded(there(*everything[j][:2]), lambda j=j: message(k, j, last).wait_send())

    def fixed_message(j):
        array = (wgt, tgt)[j % 2]
        if j < 2:
            ox, oy, oz = -1, 0, 0
            src, dst = array.at[:, pl.ds(0, 1), pl.ds(YO, cy), :], array.at[:, pl.ds(cx, 1), pl.ds(YO, cy), :]
        elif j < 4:
            ox, oy, oz = 0, -1, 0
            src, dst = array.at[:, pl.ds(0, cx), pl.ds(YO, 1), :], array.at[:, pl.ds(0, cx), pl.ds(YO + cy, 1), :]
        else:
            ox, oy, oz = 0, 0, 1
            src, dst = z_fixed.at[0], z_fixed.at[1]
        return pltpu.make_async_remote_copy(
            src_ref=src, dst_ref=dst, send_sem=fixed_send.at[j], recv_sem=fixed_recv.at[j],
            device_id=device(ox, oy, oz), device_id_type=MESH), there(ox, oy), there(-ox, -oy)

    others = [(x, y, z) for z in range(nz) for y in range(ny) for x in range(nx) if (x, y, z) != (0, 0, 0)]

    def peer(x, y, z):
        return {"gx": lax.rem(gx + x, nx) if x else gx, "gy": lax.rem(gy + y, ny) if y else gy,
                "gz": lax.rem(gz + z, nz) if z else gz}

    def start_sum(k):
        for j, offset in enumerate(others):
            pltpu.make_async_remote_copy(
                src_ref=own.at[k], dst_ref=got.at[k, j], send_sem=sum_send.at[k], recv_sem=sum_recv.at[k],
                device_id=peer(*offset), device_id_type=MESH).start()

    def whole_sum(k):
        return pltpu.make_async_remote_copy(
            src_ref=got.at[k], dst_ref=got.at[k], send_sem=sum_send.at[k], recv_sem=sum_recv.at[k],
            device_id=peer(1, 0, 0), device_id_type=MESH)

    def on_line(x, y, z):
        return {"gx": x, "gy": y, "gz": z}

    pair, quad, chip_z = lax.rem(gx, 2), lax.rem(lax.div(gx, 2), 2), lax.div(gx, 4)
    line_x = [on_line(gx + c - 2 * c * pair, lax.rem(gy + s, ny), gz)
              for s in range(ny) for c in range(2) if (c, s) != (0, 0)]
    line_y = [on_line(gx + 2 * h - 4 * h * quad, gy, gz + s - 2 * s * gz)
              for s in range(nz) for h in range(2) if (h, s) != (0, 0)]
    line_z = [on_line(lax.rem(gx + 4 * s, nx), gy, gz) for s in range(1, nx // 4)]

    def tell(sem, line):
        for device in line:
            pl.semaphore_signal(sem, 1, device_id=device, device_id_type=MESH)

    inner = pl.ds(YO, cy)
    loads = [pltpu.make_async_copy(models.at[m], field.at[0, pl.ds(XO, cx), m, inner, :], load_sem.at[m]) for m in range(MODELS)]
    loads.append(pltpu.make_async_copy(targets, tgt.at[:, pl.ds(0, cx), inner, :], load_sem.at[2]))
    loads.append(pltpu.make_async_copy(weights, wgt.at[:, pl.ds(0, cx), inner, :], load_sem.at[3]))
    for copy in loads:
        copy.start()

    zero = jnp.zeros((8, cz), jnp.float32)

    def clear_planes(start, count, side):
        for k in range(ITERS + 1):
            for x in range(start, start + count):
                for m in range(MODELS):
                    for r in range(0, rows, 8):
                        field[k, x, m, pl.ds(r, 8), :] = zero
            for oz in range(2):
                x_got[k, side, oz] = zero

    def clear_rows(start):
        def clear(x, _):
            for k in range(ITERS + 1):
                for m in range(MODELS):
                    field[k, x, m, pl.ds(start, 8), :] = zero
            return 0

        lax.fori_loop(0, cx + LOW + HIGH, clear, 0)
        for k in range(ITERS + 1):
            for m in range(MODELS):
                z_own[k, m, pl.ds(start, 8), :] = zero
                z_got[k, m, pl.ds(start, 8), :] = zero

    def clear_corner(j):
        for k in range(ITERS + 1):
            for m in range(MODELS):
                corner[k, j, m] = zero

    for j, (ox, oy, _) in enumerate(corners):
        pl.when(jnp.logical_not(there(-ox, -oy)))(functools.partial(clear_corner, j))
    pl.when(gx == 0)(lambda: clear_planes(0, LOW, 0))
    pl.when(gx == nx - 1)(lambda: clear_planes(XO + cx, HIGH, 1))
    pl.when(gy == 0)(lambda: clear_rows(0))
    pl.when(gy == ny - 1)(lambda: clear_rows(rows - 8))

    barrier = pltpu.get_barrier_semaphore()
    expected = len(line_x) + len(line_y) + len(line_z)
    for ox, oy, oz in dict.fromkeys(everything):
        ok = there(ox, oy)
        guarded(ok, lambda ox=ox, oy=oy, oz=oz: pl.semaphore_signal(
            barrier, 1, device_id=device(ox, oy, oz), device_id_type=MESH))
        expected = expected + (1 if ok is None else ok.astype(jnp.int32))
    for line in (line_x, line_y, line_z):
        tell(barrier, line)

    lane = lax.broadcasted_iota(jnp.int32, (8, cz), 1)
    first, last_lane = lane == 0, lane == cz - 1
    ghost_lane = lane == jnp.where(gz == 0, 0, cz - 1)
    upward = 1 - 2 * gz
    beyond = (lax.rem(lane, SPAN) - 2) * upward >= 0
    beyond_x = (lax.rem(lax.rem(lane, 16), SPAN) - 2) * upward >= 0
    to_own = jnp.where(gz == 0, cz - 1, 1)

    def turn(v, shift):
        if isinstance(shift, int):
            shift = shift % cz
            return v if shift == 0 else pltpu.roll(v, shift, 1)
        return pltpu.roll(v, shift, 1)

    def edge(lines, x):
        return jnp.where(ghost_lane, turn(lines, lax.rem(2 * cz - SPAN * (x + 2) - 2 - gz, cz)), 0.0)

    def z_pair(v, e):
        return turn(jnp.where(first, e, v), cz - 1), turn(jnp.where(last_lane, e, v), 1)

    def pack(acc, v, x):
        return jnp.where(lax.div(lane, SPAN) == x + 2, turn(v, lax.rem(SPAN * (x + 2) + 3 - gz, cz)), acc)

    def tile_of(k, x, m, r):
        return field[k, x + XO, m, pl.ds(YO + r, 8), :]

    def over_x(body, carry):
        def block(b, carry):
            for u in range(UNROLL):
                carry = body(b * UNROLL + u, carry)
            return carry

        return lax.fori_loop(0, cx // UNROLL, block, carry)

    def pack_all(read, write):
        def planes(x, acc):
            return tuple(pack(a, read(x, m, t), x) for a, (m, t) in zip(acc, order))

        order = [(m, t) for m in range(MODELS) for t in range(tiles)]
        for a, (m, t) in zip(over_x(planes, (zero,) * len(order)), order):
            write(m, t, a)

    def pack_field(k):
        def write(m, t, v):
            z_own[k, m, pl.ds(YO + 8 * t, 8), :] = v

        pack_all(lambda x, m, t: tile_of(k, x, m, 8 * t), write)
        high, low = zero, zero
        for m in range(MODELS):
            for t in range(tiles):
                i = m * tiles + t
                v, mine = z_own[k, m, pl.ds(YO + 8 * t, 8), :], lax.div(lane, 16) == i
                high = jnp.where(mine, turn(v, 16 * i - SPAN * cx), high)
                low = jnp.where(mine, turn(v, 16 * i - 2 * SPAN), low)
        x_own[k, 0] = high
        x_own[k, 1] = low

    def join_z(k):
        low, high = [jnp.where(beyond_x, x_got[k, side, 1], turn(x_got[k, side, 0], to_own)) for side in range(2)]

        def inside(m, r):
            return jnp.where(beyond, z_got[k, m, pl.ds(r, 8), :], turn(z_own[k, m, pl.ds(r, 8), :], to_own))

        def with_x(v, before, after):
            return jnp.where(lane < 2 * SPAN, before, jnp.where(lane < SPAN * (cx + 2), v, after))

        for m in range(MODELS):
            for t in range(tiles):
                i = m * tiles + t
                z_field[min(k, 1), m, pl.ds(YO + 8 * t, 8), :] = with_x(
                    inside(m, YO + 8 * t), turn(low, -16 * i), turn(high, SPAN * (cx + 2) - 16 * i))
            for r, oy in ((0, 1), (YO + cy, -1)):
                before, after = [turn(jnp.broadcast_to(corner[k, corners.index((ox, oy, 1)), m, pl.ds(0, 1), :], (8, cz)),
                                      -ox * SPAN * cx) for ox in (1, -1)]
                z_field[min(k, 1), m, pl.ds(r, 8), :] = with_x(inside(m, r), before, after)

    def cross_part(a, b, i):
        j, l = (i + 1) % 3, (i + 2) % 3
        return a[j] * b[l] - a[l] * b[j]

    def flux_part(g1, g2, which):
        crossed = [None if i == which else cross_part(g1, g2, i) for i in range(3)]
        return [(cross_part(g2, crossed, i), cross_part(crossed, g1, i)) for i in (range(3) if which is None else [which])]

    for copy in loads[:MODELS]:
        copy.wait()
    pack_field(0)
    pl.semaphore_wait(barrier, expected)
    start_copies(0, through_z)
    start_copies(0, plain)
    tell(enter_sem.at[0], line_y)
    for copy in loads[MODELS:]:
        copy.wait()
    for a, array in enumerate((wgt, tgt)):
        def write(m, t, v, a=a):
            z_fixed[0, a, m, pl.ds(8 * t, 8), :] = v

        pack_all(lambda x, m, t, array=array: array[m, x, pl.ds(YO + 8 * t, 8), :], write)
    fixed = [fixed_message(j) for j in range(5)]
    for copy, sends, _ in fixed:
        guarded(sends, copy.start)
    wait_copies(0, through_z)
    join_z(0)
    wait_copies(0, plain)
    pl.semaphore_wait(enter_sem.at[0], len(line_y))
    tell(enter_sem.at[1], line_z)
    for copy, _, receives in fixed:
        guarded(receives, copy.wait_recv)

    for k in range(1, ITERS + 1):
        final = k == ITERS
        for j in range(wide):
            grads = []
            for m in range(MODELS):
                here = z_field[0, m, pl.ds(YO - 1 + 8 * j, 8), :]
                grads.append([turn(here, -SPAN) - turn(here, SPAN),
                              z_field[0, m, pl.ds(YO + 8 * j, 8), :] - z_field[0, m, pl.ds(YO - 2 + 8 * j, 8), :],
                              turn(here, -1) - turn(here, 1)])
            for i, parts in enumerate(flux_part(grads[0], grads[1], None)):
                for m in range(MODELS):
                    z_flux[i, m, pl.ds(YO - 1 + 8 * j, 8), :] = parts[m]

        for x in (-1, cx + 1):
            for j in range(wide):
                grads = []
                for m in range(MODELS):
                    here = tile_of(0, x, m, 8 * j - 1)
                    up, down = z_pair(here, edge(z_field[0, m, pl.ds(YO - 1 + 8 * j, 8), :], x))
                    grads.append([tile_of(0, x + 1, m, 8 * j - 1) - tile_of(0, x - 1, m, 8 * j - 1),
                                  tile_of(0, x, m, 8 * j) - tile_of(0, x, m, 8 * j - 2), up - down])
                parts = flux_part(grads[0], grads[1], 0)[0]
                for m in range(MODELS):
                    flux0[x + 1, m, pl.ds(YO - 1 + 8 * j, 8), :] = parts[m]

        def fluxes(x, carry):
            for j in range(wide):
                grads = []
                at = pl.ds(YO - 1 + 8 * j, 8)
                for m in range(MODELS):
                    here = tile_of(0, x, m, 8 * j - 1)
                    up, down = z_pair(here, edge(z_field[0, m, at, :], x))
                    xp, xm = tile_of(0, x + 1, m, 8 * j - 1), tile_of(0, x - 1, m, 8 * j - 1)
                    yp, ym = tile_of(0, x, m, 8 * j), tile_of(0, x, m, 8 * j - 2)
                    grads.append([xp - xm, yp - ym, up - down])
                    smooth = 6.0 * here - ((xp + xm) + (yp + ym) + (up + down))
                    base[m, x, at, :] = wgt[m, x, at, :] * (here - tgt[m, x, at, :]) + smooth
                parts = flux_part(grads[0], grads[1], None)
                for m in range(MODELS):
                    flux0[x + 1, m, at, :] = parts[0][m]
                    flux1[x, m, at, :] = parts[1][m]
                    flux2[x, m, at, :] = parts[2][m]
            return carry

        over_x(fluxes, 0)
        fluxes(cx, 0)

        def no_plane(x):
            for m in range(MODELS):
                for r in range(0, rows, 8):
                    flux0[x + 1, m, pl.ds(r, 8), :] = zero

        def no_row(y):
            for x in range(cx + 1):
                for m in range(MODELS):
                    flux1[x, m, pl.ds(YO + y, 1), :] = zero[0:1]

        pl.when(gx == 0)(lambda: no_plane(-1))
        pl.when(gx == nx - 1)(lambda: no_plane(cx))
        pl.when(gy == 0)(lambda: no_row(-1))
        pl.when(gy == ny - 1)(lambda: no_row(cy))

        def gradient(x, m, r):
            at = pl.ds(YO + r, 8)
            here = flux2[x, m, at, :]
            up, down = z_pair(here, edge(z_flux[2, m, at, :], x))
            div = (flux0[x + 2, m, at, :] - flux0[x, m, at, :]
                   + (flux1[x, m, pl.ds(YO + r + 1, 8), :] - flux1[x, m, pl.ds(YO + r - 1, 8), :]) + (up - down))
            return base[m, x, at, :] + KAPPA * div

        def gradients(x, norm):
            for t in range(tiles):
                for m in range(MODELS):
                    grad = gradient(x, m, 8 * t)
                    field[k, x + XO, m, pl.ds(YO + 8 * t, 8), :] = grad
                    norm = norm + grad * grad
            return norm

        norm = over_x(gradients, zero)

        def x_face():
            for t in range(tiles):
                for m in range(MODELS):
                    field[k, cx + XO, m, pl.ds(YO + 8 * t, 8), :] = gradient(cx, m, 8 * t)

        def y_face():
            def row_of(x, carry):
                for m in range(MODELS):
                    field[k, x + XO, m, pl.ds(YO + cy, 1), :] = gradient(x, m, cy)[0:1]
                return carry

            over_x(row_of, 0)

        pl.when(gx < nx - 1)(x_face)
        pl.when(gy < ny - 1)(y_face)
        start_copies(k, [0, 2] if final else plain, final)

        for t in range(tiles):
            for m in range(MODELS):
                def shifted(ref, i, dy=0):
                    return ref[i, m, pl.ds(YO + 8 * t + dy, 8), :]

                here, f0, f2 = shifted(z_field, 0), shifted(z_flux, 0), shifted(z_flux, 2)
                div = (turn(f0, -SPAN) - turn(f0, SPAN) + (shifted(z_flux, 1, 1) - shifted(z_flux, 1, -1))
                       + (turn(f2, -1) - turn(f2, 1)))
                around = ((turn(here, -SPAN) + turn(here, SPAN)) + (shifted(z_field, 0, 1) + shifted(z_field, 0, -1))
                          + (turn(here, -1) + turn(here, 1)))
                misfit = z_fixed[1, 0, m, pl.ds(8 * t, 8), :] * (here - z_fixed[1, 1, m, pl.ds(8 * t, 8), :])
                z_grad[m, pl.ds(YO + 8 * t, 8), :] = misfit + (6.0 * here - around) + KAPPA * div

        inside_up = (gz == 0).astype(jnp.float32)

        def curves(x, curve):
            for t in range(tiles):
                for m in range(MODELS):
                    here = tile_of(k, x, m, 8 * t)
                    e = edge(z_grad[m, pl.ds(YO + 8 * t, 8), :], x) * inside_up
                    up = turn(jnp.where(first, e, here), cz - 1)
                    pairs = tile_of(k, x + 1, m, 8 * t) + tile_of(k, x, m, 8 * t + 1) + up
                    curve = curve + here * ((wgt[m, x, pl.ds(YO + 8 * t, 8), :] + 6.0) * here - 2.0 * pairs)
            return curve

        curve = over_x(curves, zero)

        def fold(v):
            return jnp.sum(v, axis=0, keepdims=True)

        own[k - 1, pl.ds(0, 1), :] = fold(norm)
        own[k - 1, pl.ds(1, 1), :] = fold(curve)
        if k == 1:
            pl.semaphore_wait(enter_sem.at[1], len(line_z))
        start_sum(k - 1)
        if final:
            wait_copies(k, [0, 2], True)

            def applies(x, carry):
                for t in range(tiles):
                    for m in range(MODELS):
                        here = tile_of(k, x, m, 8 * t)
                        up, down = z_pair(here, edge(z_grad[m, pl.ds(YO + 8 * t, 8), :], x))
                        around = ((tile_of(k, x + 1, m, 8 * t) + tile_of(k, x - 1, m, 8 * t))
                                  + (tile_of(k, x, m, 8 * t + 1) + tile_of(k, x, m, 8 * t - 1)) + (up + down))
                        applied_out[m, x, pl.ds(8 * t, 8), :] = (
                            wgt[m, x, pl.ds(YO + 8 * t, 8), :] * here + (6.0 * here - around))
                return carry

            over_x(applies, 0)
        else:
            pack_field(k)
            start_copies(k, through_z)
            wait_copies(k, through_z)
            join_z(k)
            wait_copies(k, plain)
        whole_sum(k - 1).wait_recv()
        partial = [own[k - 1]] + [got[k - 1, j] for j in range(len(others))]
        while len(partial) > 1:
            partial = [sum(partial[i:i + 2]) for i in range(0, len(partial), 2)]
        sums = jnp.sum(partial[0], axis=1, keepdims=True)
        alpha = jnp.broadcast_to(sums[0:1] / sums[1:2], (8, cz))

        if k == 1:
            wait_sent(0, plain + through_z)
            for copy, sends, _ in fixed:
                guarded(sends, copy.wait_send)
        if final:
            wait_sent(k, [0, 2], True)
        else:
            wait_sent(k, plain + through_z)
        whole_sum(k - 1).wait_send()

        if final:
            def step(x, carry):
                for m in range(MODELS):
                    for t in range(tiles):
                        updated[m, x, pl.ds(8 * t, 8), :] = tile_of(0, x, m, 8 * t) - alpha * tile_of(k, x, m, 8 * t)
                return carry

            over_x(step, 0)
        else:
            def step(x, carry):
                for m in range(MODELS):
                    for r in range(0, rows, 8):
                        field[0, x, m, pl.ds(r, 8), :] = (
                            field[0, x, m, pl.ds(r, 8), :] - alpha * field[k, x, m, pl.ds(r, 8), :])
                return carry

            lax.fori_loop(0, cx + LOW + HIGH, step, 0)
            for m in range(MODELS):
                for r in range(0, rows, 8):
                    z_field[0, m, pl.ds(r, 8), :] = z_field[0, m, pl.ds(r, 8), :] - alpha * z_field[1, m, pl.ds(r, 8), :]


def solution(mesh):
    sizes = (mesh.shape["gx"], mesh.shape["gy"], mesh.shape["gz"])
    nx, ny, nz = sizes

    def local(models, targets, weights):
        _, cx, cy, cz = models.shape
        assert nz == 2 and nx % 4 == 0 and cy % 8 == 0
        assert SPAN * (cx + 4) <= cz and 16 * MODELS * (cy // 8) <= cz
        f32 = jnp.float32
        rows = YO + cy + 8
        others = nx * ny * nz - 1

        def vmem(*shape):
            return pltpu.VMEM(shape, f32)

        return pl.pallas_call(
            functools.partial(kernel, sizes),
            out_shape=[jax.ShapeDtypeStruct(models.shape, f32)] * 2,
            in_specs=[pl.BlockSpec(memory_space=pltpu.HBM)] * 3,
            out_specs=[pl.BlockSpec(memory_space=pltpu.VMEM)] * 2,
            scratch_shapes=[
                vmem(ITERS + 1, cx + LOW + HIGH, MODELS, rows, cz),
                vmem(MODELS, cx + 1, rows, cz),
                vmem(MODELS, cx + 1, rows, cz),
                vmem(MODELS, cx + 1, rows, cz),
                vmem(cx + 3, MODELS, rows, cz),
                vmem(cx + 1, MODELS, rows + 8, cz),
                vmem(cx + 1, MODELS, rows, cz),
                vmem(ITERS + 1, MODELS, rows, cz),
                vmem(ITERS + 1, MODELS, rows, cz),
                vmem(2, MODELS, rows, cz),
                vmem(3, MODELS, rows, cz),
                vmem(MODELS, rows, cz),
                vmem(2, 2, MODELS, cy, cz),
                vmem(ITERS + 1, 2, 8, cz),
                vmem(ITERS + 1, 2, 2, 8, cz),
                vmem(ITERS + 1, 4, MODELS, 8, cz),
                vmem(ITERS, 2, cz),
                vmem(ITERS, others, 2, cz),
                pltpu.SemaphoreType.DMA((4,)),
                pltpu.SemaphoreType.DMA((ITERS + 1, 21)),
                pltpu.SemaphoreType.DMA((ITERS + 1, 21)),
                pltpu.SemaphoreType.DMA((5,)),
                pltpu.SemaphoreType.DMA((5,)),
                pltpu.SemaphoreType.DMA((ITERS,)),
                pltpu.SemaphoreType.DMA((ITERS,)),
                pltpu.SemaphoreType.REGULAR((2,)),
            ],
            compiler_params=pltpu.CompilerParams(
                collective_id=0, has_side_effects=True, vmem_limit_bytes=24 * 2**20),
        )(*[pltpu.with_memory_space_constraint(a, pltpu.HBM) for a in (models, targets, weights)])

    spec = P(None, "gx", "gy", "gz")
    return jax.shard_map(local, mesh=mesh, in_specs=(spec,) * 3, out_specs=(spec,) * 2, check_vma=False)
```

time: 58 us -> 53.6 us (0.924)
  Pallas kernels: 55.7 us -> 51.2 us
    pallas_call x1, Pallas kernels: 55.7 us -> 51.2 us  [local(): pl.pallas_call(functools.partial(kernel, sizes), out_shape=[jax.ShapeDtyp...]
where the time goes in v3:
time: 53.6 us; the launch traced here: 53.5 us
  Pallas kernels  51.2 us (96%)
  local copies, waits for them, and re-layouts  1.59 us (3%)
  between operations  0.64 us (1%)
    pallas_call x1, Pallas kernels, local(): pl.pallas_call(functools.partial(kernel, sizes), out_shape=[jax.ShapeDtyp...  51.2 us
    unnamed x2, local copies, waits for them, and re-layouts  1.59 us

profile of v3, /device:TPU:1, one launch (start us, length us, event | category | flops | bytes accessed | tf_op | source)
XLA Modules:
  0.0 53.5 jit_solution(15721400324396670208)
XLA Ops:
  0.6 51.2 %shard_map.50 = (f32[2,16,32,128]{3,2,1,0:T(8,128)S(1)}, f32[2,16,32,128]{3,2,1,0:T(8,128)S(1)}) custom-call(f32[2,16,32,128]{3,2,1,0:T(8,128)} %models.1, f32[2,16,32,128]{3,2,1,0:T(8,128)} %targets.1, f32[2,16,32,128]{3,2,1,0:T(8,128)} %weights.1), custom_call_target="tpu_custom_call" | custom-call | tf_op jit(solution)/shard_map/pallas_call | solution.py:520
  51.9 0.8 %copy.7 = f32[2,16,32,128]{3,2,1,0:T(8,128)} copy(f32[2,16,32,128]{3,2,1,0:T(8,128)S(1)} %get-tuple-element.4) | data formatting | bytes 1048576
  52.7 0.8 %copy.8 = f32[2,16,32,128]{3,2,1,0:T(8,128)} copy(f32[2,16,32,128]{3,2,1,0:T(8,128)S(1)} %get-tuple-element.5) | data formatting | bytes 1048576

commit v4 on v3

--- a/solution.py
+++ b/solution.py
@@ -14,7 +14,7 @@
 YO = 8
 LOW, HIGH = 2, 3
 SPAN = 5
-UNROLL = 4
+FLUX, GRADIENT, CURVE, PACK, APPLY, STEP = 4, 4, 8, 4, 4, 4
 KAPPA = 0.05 * -2.0 * 0.5 * 0.125
 
 
@@ -117,27 +117,35 @@
             src_ref=src, dst_ref=dst, send_sem=fixed_send.at[j], recv_sem=fixed_recv.at[j],
             device_id=device(ox, oy, oz), device_id_type=MESH), there(ox, oy), there(-ox, -oy)
 
-    others = [(x, y, z) for z in range(nz) for y in range(ny) for x in range(nx) if (x, y, z) != (0, 0, 0)]
-
-    def peer(x, y, z):
-        return {"gx": lax.rem(gx + x, nx) if x else gx, "gy": lax.rem(gy + y, ny) if y else gy,
-                "gz": lax.rem(gz + z, nz) if z else gz}
+    pair, quad, chip_z = lax.rem(gx, 2), lax.rem(lax.div(gx, 2), 2), lax.div(gx, 4)
+    turns_z = nx // 4
+
+    def hops(offset):
+        x, z, h, q, c = offset
+        return min(x, ny - x) + min(z, turns_z - z) + (1 if q else 2 * h), c
+
+    others = [(x, z, h, q, c) for x in range(ny) for z in range(turns_z) for h in range(nz) for q in range(2) for c in range(2)]
+    others = sorted(others, key=hops, reverse=True)[:-1]
+    place_x = [lax.rem(gy + x, ny) if x else gy for x in range(ny)]
+    place_h = [gz, 1 - gz]
+    place_gx = {(z, q, c): 4 * (lax.rem(chip_z + z, turns_z) if z else chip_z) + 2 * (1 - quad if q else quad) + (1 - pair if c else pair)
+                for z in range(turns_z) for q in range(2) for c in range(2)}
 
     def start_sum(k):
-        for j, offset in enumerate(others):
+        for j, (x, z, h, q, c) in enumerate(others):
             pltpu.make_async_remote_copy(
-                src_ref=own.at[k], dst_ref=got.at[k, j], send_sem=sum_send.at[k], recv_sem=sum_recv.at[k],
-                device_id=peer(*offset), device_id_type=MESH).start()
+                src_ref=own.at[k], dst_ref=got.at[k, pl.ds(j, 1)], send_sem=sum_send.at[k], recv_sem=sum_recv.at[k],
+                device_id={"gx": place_gx[z, q, c], "gy": place_x[x], "gz": place_h[h]}, device_id_type=MESH).start()
 
     def whole_sum(k):
+        landed = got.at[k, pl.ds(0, len(others))]
         return pltpu.make_async_remote_copy(
-            src_ref=got.at[k], dst_ref=got.at[k], send_sem=sum_send.at[k], recv_sem=sum_recv.at[k],
-            device_id=peer(1, 0, 0), device_id_type=MESH)
+            src_ref=landed, dst_ref=landed, send_sem=sum_send.at[k], recv_sem=sum_recv.at[k],
+            device_id={"gx": gx, "gy": gy, "gz": 1 - gz}, device_id_type=MESH)
 
     def on_line(x, y, z):
         return {"gx": x, "gy": y, "gz": z}
 
-    pair, quad, chip_z = lax.rem(gx, 2), lax.rem(lax.div(gx, 2), 2), lax.div(gx, 4)
     line_x = [on_line(gx + c - 2 * c * pair, lax.rem(gy + s, ny), gz)
               for s in range(ny) for c in range(2) if (c, s) != (0, 0)]
     line_y = [on_line(gx + 2 * h - 4 * h * quad, gy, gz + s - 2 * s * gz)
@@ -227,20 +235,20 @@
     def tile_of(k, x, m, r):
         return field[k, x + XO, m, pl.ds(YO + r, 8), :]
 
-    def over_x(body, carry):
+    def over_x(body, carry, unroll):
         def block(b, carry):
-            for u in range(UNROLL):
-                carry = body(b * UNROLL + u, carry)
+            for u in range(unroll):
+                carry = body(b * unroll + u, carry)
             return carry
 
-        return lax.fori_loop(0, cx // UNROLL, block, carry)
+        return lax.fori_loop(0, cx // unroll, block, carry)
 
     def pack_all(read, write):
         def planes(x, acc):
             return tuple(pack(a, read(x, m, t), x) for a, (m, t) in zip(acc, order))
 
         order = [(m, t) for m in range(MODELS) for t in range(tiles)]
-        for a, (m, t) in zip(over_x(planes, (zero,) * len(order)), order):
+        for a, (m, t) in zip(over_x(planes, (zero,) * len(order), PACK), order):
             write(m, t, a)
 
     def pack_field(k):
@@ -354,8 +362,8 @@
                     flux2[x, m, at, :] = parts[2][m]
             return carry
 
-        over_x(fluxes, 0)
         fluxes(cx, 0)
+        over_x(fluxes, 0, FLUX)
 
         def no_plane(x):
             for m in range(MODELS):
@@ -386,27 +394,18 @@
                     grad = gradient(x, m, 8 * t)
                     field[k, x + XO, m, pl.ds(YO + 8 * t, 8), :] = grad
                     norm = norm + grad * grad
+            for m in range(MODELS):
+                grad = gradient(x, m, cy)[0:1]
+                field[k, x + XO, m, pl.ds(YO + cy, 1), :] = jnp.where(gy < ny - 1, grad, 0.0)
             return norm
 
-        norm = over_x(gradients, zero)
-
-        def x_face():
-            for t in range(tiles):
-                for m in range(MODELS):
-                    field[k, cx + XO, m, pl.ds(YO + 8 * t, 8), :] = gradient(cx, m, 8 * t)
-
-        def y_face():
-            def row_of(x, carry):
-                for m in range(MODELS):
-                    field[k, x + XO, m, pl.ds(YO + cy, 1), :] = gradient(x, m, cy)[0:1]
-                return carry
-
-            over_x(row_of, 0)
-
-        pl.when(gx < nx - 1)(x_face)
-        pl.when(gy < ny - 1)(y_face)
-        start_copies(k, [0, 2] if final else plain, final)
-
+        norm = over_x(gradients, zero, GRADIENT)
+
+        if final:
+            start_copies(k, [0, 2], True)
+        for t in range(tiles):
+            for m in range(MODELS):
+                field[k, cx + XO, m, pl.ds(YO + 8 * t, 8), :] = jnp.where(gx < nx - 1, gradient(cx, m, 8 * t), 0.0)
         for t in range(tiles):
             for m in range(MODELS):
                 def shifted(ref, i, dy=0):
@@ -432,13 +431,15 @@
                     curve = curve + here * ((wgt[m, x, pl.ds(YO + 8 * t, 8), :] + 6.0) * here - 2.0 * pairs)
             return curve
 
-        curve = over_x(curves, zero)
+        curve = over_x(curves, zero, CURVE)
 
         def fold(v):
-            return jnp.sum(v, axis=0, keepdims=True)
-
-        own[k - 1, pl.ds(0, 1), :] = fold(norm)
-        own[k - 1, pl.ds(1, 1), :] = fold(curve)
+            v = jnp.sum(v, axis=0, keepdims=True)
+            return v + turn(v, cz // 2)
+
+        both = jnp.where(lane[0:1] < cz // 2, fold(norm), fold(curve))
+        own[k - 1] = both
+        got[k - 1, pl.ds(len(others), 1), :] = both
         if k == 1:
             pl.semaphore_wait(enter_sem.at[1], len(line_z))
         start_sum(k - 1)
@@ -456,19 +457,22 @@
                             wgt[m, x, pl.ds(YO + 8 * t, 8), :] * here + (6.0 * here - around))
                 return carry
 
-            over_x(applies, 0)
+            over_x(applies, 0, APPLY)
         else:
+            start_copies(k, plain)
             pack_field(k)
             start_copies(k, through_z)
             wait_copies(k, through_z)
             join_z(k)
             wait_copies(k, plain)
         whole_sum(k - 1).wait_recv()
-        partial = [own[k - 1]] + [got[k - 1, j] for j in range(len(others))]
+        partial = [got[k - 1, pl.ds(r, 8), :] for r in range(0, len(others) + 1, 8)]
         while len(partial) > 1:
             partial = [sum(partial[i:i + 2]) for i in range(0, len(partial), 2)]
-        sums = jnp.sum(partial[0], axis=1, keepdims=True)
-        alpha = jnp.broadcast_to(sums[0:1] / sums[1:2], (8, cz))
+        half = lane < cz // 2
+        sums = [jnp.sum(jnp.sum(jnp.where(half, *terms), axis=0, keepdims=True), axis=1, keepdims=True)
+                for terms in ((partial[0], 0.0), (0.0, partial[0]))]
+        alpha = jnp.broadcast_to(sums[0] / sums[1], (8, cz))
 
         if k == 1:
             wait_sent(0, plain + through_z)
@@ -487,7 +491,7 @@
                         updated[m, x, pl.ds(8 * t, 8), :] = tile_of(0, x, m, 8 * t) - alpha * tile_of(k, x, m, 8 * t)
                 return carry
 
-            over_x(step, 0)
+            over_x(step, 0, STEP)
         else:
             def step(x, carry):
                 for m in range(MODELS):
@@ -512,7 +516,6 @@
         assert SPAN * (cx + 4) <= cz and 16 * MODELS * (cy // 8) <= cz
         f32 = jnp.float32
         rows = YO + cy + 8
-        others = nx * ny * nz - 1
 
         def vmem(*shape):
             return pltpu.VMEM(shape, f32)
@@ -539,8 +542,8 @@
                 vmem(ITERS + 1, 2, 8, cz),
                 vmem(ITERS + 1, 2, 2, 8, cz),
                 vmem(ITERS + 1, 4, MODELS, 8, cz),
-                vmem(ITERS, 2, cz),
-                vmem(ITERS, others, 2, cz),
+                vmem(ITERS, 1, cz),
+                vmem(ITERS, nx * ny * nz, cz),
                 pltpu.SemaphoreType.DMA((4,)),
                 pltpu.SemaphoreType.DMA((ITERS + 1, 21)),
                 pltpu.SemaphoreType.DMA((ITERS + 1, 21)),

time: 53.6 us -> 48.4 us (0.903)
  Pallas kernels: 51.2 us -> 46 us
    pallas_call x1, Pallas kernels: 51.2 us -> 46 us  [local(): pl.pallas_call(functools.partial(kernel, sizes), out_shape=[jax.ShapeDtyp...]
where the time goes in v4:
time: 48.4 us; the launch traced here: 48.3 us
  Pallas kernels  46 us (95%)
  local copies, waits for them, and re-layouts  1.59 us (3%)
  between operations  0.64 us (1%)
    pallas_call x1, Pallas kernels, local(): pl.pallas_call(functools.partial(kernel, sizes), out_shape=[jax.ShapeDtyp...  46 us
    unnamed x2, local copies, waits for them, and re-layouts  1.59 us

profile of v4, /device:TPU:1, one launch (start us, length us, event | category | flops | bytes accessed | tf_op | source)
XLA Modules:
  0.0 48.3 jit_solution(3425569974551774804)
XLA Ops:
  0.6 46.0 %shard_map.50 = (f32[2,16,32,128]{3,2,1,0:T(8,128)S(1)}, f32[2,16,32,128]{3,2,1,0:T(8,128)S(1)}) custom-call(f32[2,16,32,128]{3,2,1,0:T(8,128)} %models.1, f32[2,16,32,128]{3,2,1,0:T(8,128)} %targets.1, f32[2,16,32,128]{3,2,1,0:T(8,128)} %weights.1), custom_call_target="tpu_custom_call" | custom-call | tf_op jit(solution)/shard_map/pallas_call | solution.py:523
  46.7 0.8 %copy.7 = f32[2,16,32,128]{3,2,1,0:T(8,128)} copy(f32[2,16,32,128]{3,2,1,0:T(8,128)S(1)} %get-tuple-element.4) | data formatting | bytes 1048576
  47.5 0.8 %copy.8 = f32[2,16,32,128]{3,2,1,0:T(8,128)} copy(f32[2,16,32,128]{3,2,1,0:T(8,128)S(1)} %get-tuple-element.5) | data formatting | bytes 1048576

commit v5 on v4

--- a/solution.py
+++ b/solution.py
@@ -211,7 +211,8 @@
 
     lane = lax.broadcasted_iota(jnp.int32, (8, cz), 1)
     first, last_lane = lane == 0, lane == cz - 1
-    ghost_lane = lane == jnp.where(gz == 0, 0, cz - 1)
+    end_lane = (1 - gz) * (cz - 1)
+    ghost_lane = lane == end_lane
     upward = 1 - 2 * gz
     beyond = (lax.rem(lane, SPAN) - 2) * upward >= 0
     beyond_x = (lax.rem(lax.rem(lane, 16), SPAN) - 2) * upward >= 0
@@ -224,10 +225,10 @@
         return pltpu.roll(v, shift, 1)
 
     def edge(lines, x):
-        return jnp.where(ghost_lane, turn(lines, lax.rem(2 * cz - SPAN * (x + 2) - 2 - gz, cz)), 0.0)
+        return jnp.where(ghost_lane, turn(lines, lax.rem(cz + end_lane - SPAN * (x + 2) - 2, cz)), 0.0)
 
     def z_pair(v, e):
-        return turn(jnp.where(first, e, v), cz - 1), turn(jnp.where(last_lane, e, v), 1)
+        return jnp.where(last_lane, e, turn(v, cz - 1)), jnp.where(first, e, turn(v, 1))
 
     def pack(acc, v, x):
         return jnp.where(lax.div(lane, SPAN) == x + 2, turn(v, lax.rem(SPAN * (x + 2) + 3 - gz, cz)), acc)
@@ -426,7 +427,7 @@
                 for m in range(MODELS):
                     here = tile_of(k, x, m, 8 * t)
                     e = edge(z_grad[m, pl.ds(YO + 8 * t, 8), :], x) * inside_up
-                    up = turn(jnp.where(first, e, here), cz - 1)
+                    up = jnp.where(last_lane, e, turn(here, cz - 1))
                     pairs = tile_of(k, x + 1, m, 8 * t) + tile_of(k, x, m, 8 * t + 1) + up
                     curve = curve + here * ((wgt[m, x, pl.ds(YO + 8 * t, 8), :] + 6.0) * here - 2.0 * pairs)
             return curve

time: 48.4 us -> 47 us (0.971)
  Pallas kernels: 46 us -> 44.6 us
    pallas_call x1, Pallas kernels: 46 us -> 44.6 us  [local(): pl.pallas_call(functools.partial(kernel, sizes), out_shape=[jax.ShapeDtyp...]
where the time goes in v5:
time: 47 us; the launch traced here: 46.8 us
  Pallas kernels  44.6 us (95%)
  local copies, waits for them, and re-layouts  1.59 us (3%)
  between operations  0.64 us (1%)
    pallas_call x1, Pallas kernels, local(): pl.pallas_call(functools.partial(kernel, sizes), out_shape=[jax.ShapeDtyp...  44.6 us
    unnamed x2, local copies, waits for them, and re-layouts  1.59 us

profile of v5, /device:TPU:1, one launch (start us, length us, event | category | flops | bytes accessed | tf_op | source)
XLA Modules:
  0.0 46.8 jit_solution(16587602312141808599)
XLA Ops:
  0.6 44.6 %shard_map.50 = (f32[2,16,32,128]{3,2,1,0:T(8,128)S(1)}, f32[2,16,32,128]{3,2,1,0:T(8,128)S(1)}) custom-call(f32[2,16,32,128]{3,2,1,0:T(8,128)} %models.1, f32[2,16,32,128]{3,2,1,0:T(8,128)} %targets.1, f32[2,16,32,128]{3,2,1,0:T(8,128)} %weights.1), custom_call_target="tpu_custom_call" | custom-call | tf_op jit(solution)/shard_map/pallas_call | solution.py:524
  45.2 0.8 %copy.7 = f32[2,16,32,128]{3,2,1,0:T(8,128)} copy(f32[2,16,32,128]{3,2,1,0:T(8,128)S(1)} %get-tuple-element.4) | data formatting | bytes 1048576
  46.0 0.8 %copy.8 = f32[2,16,32,128]{3,2,1,0:T(8,128)} copy(f32[2,16,32,128]{3,2,1,0:T(8,128)S(1)} %get-tuple-element.5) | data formatting | bytes 1048576

commit v6 on v5

--- a/solution.py
+++ b/solution.py
@@ -131,8 +131,9 @@
     place_gx = {(z, q, c): 4 * (lax.rem(chip_z + z, turns_z) if z else chip_z) + 2 * (1 - quad if q else quad) + (1 - pair if c else pair)
                 for z in range(turns_z) for q in range(2) for c in range(2)}
 
-    def start_sum(k):
-        for j, (x, z, h, q, c) in enumerate(others):
+    def start_sum(k, which):
+        for j in which:
+            x, z, h, q, c = others[j]
             pltpu.make_async_remote_copy(
                 src_ref=own.at[k], dst_ref=got.at[k, pl.ds(j, 1)], send_sem=sum_send.at[k], recv_sem=sum_recv.at[k],
                 device_id={"gx": place_gx[z, q, c], "gy": place_x[x], "gz": place_h[h]}, device_id_type=MESH).start()
@@ -443,7 +444,13 @@
         got[k - 1, pl.ds(len(others), 1), :] = both
         if k == 1:
             pl.semaphore_wait(enter_sem.at[1], len(line_z))
-        start_sum(k - 1)
+        far_ones = len(others) * 2 // 3
+        start_sum(k - 1, range(far_ones))
+        if not final:
+            start_copies(k, plain)
+            pack_field(k)
+            start_copies(k, through_z)
+        start_sum(k - 1, range(far_ones, len(others)))
         if final:
             wait_copies(k, [0, 2], True)
 
@@ -460,9 +467,6 @@
 
             over_x(applies, 0, APPLY)
         else:
-            start_copies(k, plain)
-            pack_field(k)
-            start_copies(k, through_z)
             wait_copies(k, through_z)
             join_z(k)
             wait_copies(k, plain)
@@ -507,6 +511,14 @@
                     z_field[0, m, pl.ds(r, 8), :] = z_field[0, m, pl.ds(r, 8), :] - alpha * z_field[1, m, pl.ds(r, 8), :]
 
 
+def store(updated, applied, updated_out, applied_out, sems):
+    copies = [pltpu.make_async_copy(updated, updated_out, sems.at[0]), pltpu.make_async_copy(applied, applied_out, sems.at[1])]
+    for copy in copies:
+        copy.start()
+    for copy in copies:
+        copy.wait()
+
+
 def solution(mesh):
     sizes = (mesh.shape["gx"], mesh.shape["gy"], mesh.shape["gz"])
     nx, ny, nz = sizes
@@ -521,7 +533,7 @@
         def vmem(*shape):
             return pltpu.VMEM(shape, f32)
 
-        return pl.pallas_call(
+        results = pl.pallas_call(
             functools.partial(kernel, sizes),
             out_shape=[jax.ShapeDtypeStruct(models.shape, f32)] * 2,
             in_specs=[pl.BlockSpec(memory_space=pltpu.HBM)] * 3,
@@ -557,6 +569,13 @@
             compiler_params=pltpu.CompilerParams(
                 collective_id=0, has_side_effects=True, vmem_limit_bytes=24 * 2**20),
         )(*[pltpu.with_memory_space_constraint(a, pltpu.HBM) for a in (models, targets, weights)])
+        return pl.pallas_call(
+            store,
+            out_shape=[jax.ShapeDtypeStruct(models.shape, f32)] * 2,
+            in_specs=[pl.BlockSpec(memory_space=pltpu.VMEM)] * 2,
+            out_specs=[pl.BlockSpec(memory_space=pltpu.HBM)] * 2,
+            scratch_shapes=[pltpu.SemaphoreType.DMA((2,))],
+        )(*[pltpu.with_memory_space_constraint(a, pltpu.VMEM) for a in results])
 
     spec = P(None, "gx", "gy", "gz")
     return jax.shard_map(local, mesh=mesh, in_specs=(spec,) * 3, out_specs=(spec,) * 2, check_vma=False)

time: 47 us -> 46.1 us (0.981)
  local copies, waits for them, and re-layouts: 1.59 us -> 0 us
  Pallas kernels: 44.6 us -> 45.4 us
    unnamed x2 -> x0, local copies, waits for them, and re-layouts: 1.59 us -> none
    pallas_call x0 -> x1, Pallas kernels: none -> 0.99 us  [local(): pl.pallas_call(store, out_shape=[jax.ShapeDtypeStruct(models.shape, f32)]...]
where the time goes in v6:
time: 46.1 us; the launch traced here: 46 us
  Pallas kernels  45.4 us (98%)
  between operations  0.64 us (1%)
    pallas_call x1, Pallas kernels, local(): pl.pallas_call(functools.partial(kernel, sizes), out_shape=[jax.ShapeDtyp...  44.4 us
    pallas_call x1, Pallas kernels, local(): pl.pallas_call(store, out_shape=[jax.ShapeDtypeStruct(models.shape, f32)]...  0.99 us

profile of v6, /device:TPU:1, one launch (start us, length us, event | category | flops | bytes accessed | tf_op | source)
XLA Modules:
  0.0 46.0 jit_solution(8564594607994403698)
XLA Ops:
  0.6 44.4 %shard_map.50 = (f32[2,16,32,128]{3,2,1,0:T(8,128)S(1)}, f32[2,16,32,128]{3,2,1,0:T(8,128)S(1)}) custom-call(f32[2,16,32,128]{3,2,1,0:T(8,128)} %models.1, f32[2,16,32,128]{3,2,1,0:T(8,128)} %targets.1, f32[2,16,32,128]{3,2,1,0:T(8,128)} %weights.1), custom_call_target="tpu_custom_call" | custom-call | tf_op jit(solution)/shard_map/pallas_call | solution.py:536
  45.0 1.0 %shard_map.51 = (f32[2,16,32,128]{3,2,1,0:T(8,128)}, f32[2,16,32,128]{3,2,1,0:T(8,128)}) custom-call(f32[2,16,32,128]{3,2,1,0:T(8,128)S(1)} %get-tuple-element.4.updated, f32[2,16,32,128]{3,2,1,0:T(8,128)S(1)} %get-tuple-element.5.applied), custom_call_target="tpu_custom_call" | custom-call | tf_op jit(solution)/shard_map/pallas_call | solution.py:572

commit v7 on v6

--- a/solution.py
+++ b/solution.py
@@ -14,7 +14,7 @@
 YO = 8
 LOW, HIGH = 2, 3
 SPAN = 5
-FLUX, GRADIENT, CURVE, PACK, APPLY, STEP = 4, 4, 8, 4, 4, 4
+FLUX, GRADIENT, CURVE, PACK, APPLY, STEP = 4, 4, 16, 4, 4, 8
 KAPPA = 0.05 * -2.0 * 0.5 * 0.125
 
 
@@ -470,15 +470,6 @@
             wait_copies(k, through_z)
             join_z(k)
             wait_copies(k, plain)
-        whole_sum(k - 1).wait_recv()
-        partial = [got[k - 1, pl.ds(r, 8), :] for r in range(0, len(others) + 1, 8)]
-        while len(partial) > 1:
-            partial = [sum(partial[i:i + 2]) for i in range(0, len(partial), 2)]
-        half = lane < cz // 2
-        sums = [jnp.sum(jnp.sum(jnp.where(half, *terms), axis=0, keepdims=True), axis=1, keepdims=True)
-                for terms in ((partial[0], 0.0), (0.0, partial[0]))]
-        alpha = jnp.broadcast_to(sums[0] / sums[1], (8, cz))
-
         if k == 1:
             wait_sent(0, plain + through_z)
             for copy, sends, _ in fixed:
@@ -488,6 +479,14 @@
         else:
             wait_sent(k, plain + through_z)
         whole_sum(k - 1).wait_send()
+        whole_sum(k - 1).wait_recv()
+        partial = [got[k - 1, pl.ds(r, 8), :] for r in range(0, len(others) + 1, 8)]
+        while len(partial) > 1:
+            partial = [sum(partial[i:i + 2]) for i in range(0, len(partial), 2)]
+        half = lane < cz // 2
+        sums = [jnp.sum(jnp.sum(jnp.where(half, *terms), axis=0, keepdims=True), axis=1, keepdims=True)
+                for terms in ((partial[0], 0.0), (0.0, partial[0]))]
+        alpha = jnp.broadcast_to(sums[0] / sums[1], (8, cz))
 
         if final:
             def step(x, carry):
@@ -498,14 +497,15 @@
 
             over_x(step, 0, STEP)
         else:
-            def step(x, carry):
-                for m in range(MODELS):
-                    for r in range(0, rows, 8):
-                        field[0, x, m, pl.ds(r, 8), :] = (
-                            field[0, x, m, pl.ds(r, 8), :] - alpha * field[k, x, m, pl.ds(r, 8), :])
+            def step(b, carry):
+                for x in range(3):
+                    for m in range(MODELS):
+                        for r in range(0, rows, 8):
+                            field[0, 3 * b + x, m, pl.ds(r, 8), :] = (
+                                field[0, 3 * b + x, m, pl.ds(r, 8), :] - alpha * field[k, 3 * b + x, m, pl.ds(r, 8), :])
                 return carry
 
-            lax.fori_loop(0, cx + LOW + HIGH, step, 0)
+            lax.fori_loop(0, (cx + LOW + HIGH) // 3, step, 0)
             for m in range(MODELS):
                 for r in range(0, rows, 8):
                     z_field[0, m, pl.ds(r, 8), :] = z_field[0, m, pl.ds(r, 8), :] - alpha * z_field[1, m, pl.ds(r, 8), :]
@@ -526,7 +526,7 @@
     def local(models, targets, weights):
         _, cx, cy, cz = models.shape
         assert nz == 2 and nx % 4 == 0 and cy % 8 == 0
-        assert SPAN * (cx + 4) <= cz and 16 * MODELS * (cy // 8) <= cz
+        assert (cx + LOW + HIGH) % 3 == 0 and SPAN * (cx + 4) <= cz and 16 * MODELS * (cy // 8) <= cz
         f32 = jnp.float32
         rows = YO + cy + 8
 

time: 46.1 us -> 45.7 us (level)
  Pallas kernels: 45.4 us -> 44.9 us
    pallas_call x1, Pallas kernels: 44.4 us -> 43.9 us  [local(): pl.pallas_call(functools.partial(kernel, sizes), out_shape=[jax.ShapeDtyp...]
where the time goes in v7:
time: 45.7 us; the launch traced here: 45.5 us
  Pallas kernels  44.9 us (98%)
  between operations  0.64 us (1%)
    pallas_call x1, Pallas kernels, local(): pl.pallas_call(functools.partial(kernel, sizes), out_shape=[jax.ShapeDtyp...  43.9 us
    pallas_call x1, Pallas kernels, local(): pl.pallas_call(store, out_shape=[jax.ShapeDtypeStruct(models.shape, f32)]...  0.99 us

profile of v7, /device:TPU:1, one launch (start us, length us, event | category | flops | bytes accessed | tf_op | source)
XLA Modules:
  0.0 45.5 jit_solution(3153009922132875246)
XLA Ops:
  0.6 43.9 %shard_map.50 = (f32[2,16,32,128]{3,2,1,0:T(8,128)S(1)}, f32[2,16,32,128]{3,2,1,0:T(8,128)S(1)}) custom-call(f32[2,16,32,128]{3,2,1,0:T(8,128)} %models.1, f32[2,16,32,128]{3,2,1,0:T(8,128)} %targets.1, f32[2,16,32,128]{3,2,1,0:T(8,128)} %weights.1), custom_call_target="tpu_custom_call" | custom-call | tf_op jit(solution)/shard_map/pallas_call | solution.py:536
  44.5 1.0 %shard_map.51 = (f32[2,16,32,128]{3,2,1,0:T(8,128)}, f32[2,16,32,128]{3,2,1,0:T(8,128)}) custom-call(f32[2,16,32,128]{3,2,1,0:T(8,128)S(1)} %get-tuple-element.4.updated, f32[2,16,32,128]{3,2,1,0:T(8,128)S(1)} %get-tuple-element.5.applied), custom_call_target="tpu_custom_call" | custom-call | tf_op jit(solution)/shard_map/pallas_call | solution.py:572

commit v8 on v7

--- a/solution.py
+++ b/solution.py
@@ -14,7 +14,7 @@
 YO = 8
 LOW, HIGH = 2, 3
 SPAN = 5
-FLUX, GRADIENT, CURVE, PACK, APPLY, STEP = 4, 4, 16, 4, 4, 8
+FLUX, GRADIENT, CURVE, PACK, APPLY, STEP = 4, 4, 16, 8, 4, 8
 KAPPA = 0.05 * -2.0 * 0.5 * 0.125
 
 

time: 45.7 us -> 45.7 us (level)
  no operation moved by 1% of the time
where the time goes in v8:
time: 45.7 us; the launch traced here: 45.5 us
  Pallas kernels  44.9 us (98%)
  between operations  0.64 us (1%)
    pallas_call x1, Pallas kernels, local(): pl.pallas_call(functools.partial(kernel, sizes), out_shape=[jax.ShapeDtyp...  43.9 us
    pallas_call x1, Pallas kernels, local(): pl.pallas_call(store, out_shape=[jax.ShapeDtypeStruct(models.shape, f32)]...  0.99 us

profile of v8, /device:TPU:1, one launch (start us, length us, event | category | flops | bytes accessed | tf_op | source)
XLA Modules:
  0.0 45.5 jit_solution(18246280278244494874)
XLA Ops:
  0.6 43.9 %shard_map.50 = (f32[2,16,32,128]{3,2,1,0:T(8,128)S(1)}, f32[2,16,32,128]{3,2,1,0:T(8,128)S(1)}) custom-call(f32[2,16,32,128]{3,2,1,0:T(8,128)} %models.1, f32[2,16,32,128]{3,2,1,0:T(8,128)} %targets.1, f32[2,16,32,128]{3,2,1,0:T(8,128)} %weights.1), custom_call_target="tpu_custom_call" | custom-call | tf_op jit(solution)/shard_map/pallas_call | solution.py:536
  44.5 1.0 %shard_map.51 = (f32[2,16,32,128]{3,2,1,0:T(8,128)}, f32[2,16,32,128]{3,2,1,0:T(8,128)}) custom-call(f32[2,16,32,128]{3,2,1,0:T(8,128)S(1)} %get-tuple-element.4.updated, f32[2,16,32,128]{3,2,1,0:T(8,128)S(1)} %get-tuple-element.5.applied), custom_call_target="tpu_custom_call" | custom-call | tf_op jit(solution)/shard_map/pallas_call | solution.py:572
